TPU v7x, 8 devices: a whole 2x2x1 slice. The times are simulated.
8 devices in a mesh: tp: 2 (over z, y), dp: 4 (over x, core).
Axes of the slice: x: 2, y: 2, z: 1, core: 2. Of those that a mesh axis runs over, the one named last changes fastest.
Arguments:
- x: bfloat16 [512, 2048], P('dp')
- lengths: int32 [512], P('dp')
- cache: bfloat16 [2, 512, 512, 576], P(None, 'dp')
- attn_norm: bfloat16 [2, 2048], replicated
- ffn_norm: bfloat16 [2, 2048], replicated
- wq: bfloat16 [2, 2048, 9216], P(None, None, 'tp')
- wo: bfloat16 [2, 8192, 2048], P(None, 'tp')
- w1: bfloat16 [2, 2048, 11264], P(None, None, ('dp', 'tp'))
- w3: bfloat16 [2, 2048, 11264], P(None, None, ('dp', 'tp'))
- w2: bfloat16 [2, 11264, 2048], P(None, ('dp', 'tp'))
Outputs:
- output: bfloat16 [512, 2048], P('dp')
All inputs are finite; a program needn't handle non-finite values.
Results may differ from a plain program's by a relative error of at most 0.02.
Values are sent between devices in bfloat16 or wider.
A program may use at most 1 GiB of HBM per device.

v0:
```python
import jax
import jax.numpy as jnp
from jax import lax
from jax.sharding import PartitionSpec as P

LAT = 512
EPS = 1e-6
SCALE = 192 ** -0.5


def _rmsnorm(v, w):
    vf = v.astype(jnp.float32)
    r = lax.rsqrt(jnp.mean(vf * vf, axis=-1, keepdims=True) + EPS)
    return (vf * r * w.astype(jnp.float32)).astype(jnp.bfloat16)


def solution(mesh):
    def body(x, lengths, cache, attn_norm, ffn_norm, wq, wo, w1, w3, w2):
        nb = x.shape[0]
        n_layers, _, s_len, kv = cache.shape
        nh = wq.shape[2] // kv
        keep = (jnp.arange(s_len)[None, :] < lengths[:, None])[:, None, :]
        for l in range(n_layers):
            c = cache[l]
            h = _rmsnorm(x, attn_norm[l])
            q = jnp.dot(h, wq[l], preferred_element_type=jnp.float32).astype(jnp.bfloat16).reshape(nb, nh, kv)
            s = jnp.einsum('bhk,btk->bht', q, c, preferred_element_type=jnp.float32) * SCALE
            p = jax.nn.softmax(jnp.where(keep, s, -jnp.inf), axis=-1).astype(jnp.bfloat16)
            o = jnp.einsum('bht,btk->bhk', p, c[:, :, :LAT], preferred_element_type=jnp.float32)
            o = o.astype(jnp.bfloat16).reshape(nb, nh * LAT)
            attn = lax.psum(jnp.dot(o, wo[l], preferred_element_type=jnp.float32), 'tp')
            x = x + attn.astype(jnp.bfloat16)
            g = _rmsnorm(x, ffn_norm[l])
            gg = lax.all_gather(g, 'dp', axis=0, tiled=True)
            u = jnp.dot(gg, w3[l], preferred_element_type=jnp.float32)
            v = jnp.dot(gg, w1[l], preferred_element_type=jnp.float32)
            a = (jax.nn.silu(u) * v).astype(jnp.bfloat16)
            yp = jnp.dot(a, w2[l], preferred_element_type=jnp.float32)
            y = lax.psum_scatter(yp, 'dp', scatter_dimension=0, tiled=True)
            y = lax.psum(y, 'tp')
            x = x + y.astype(jnp.bfloat16)
        return x

    in_specs = (
        P('dp', None),
        P('dp'),
        P(None, 'dp', None, None),
        P(None, None),
        P(None, None),
        P(None, None, 'tp'),
        P(None, 'tp', None),
        P(None, None, ('dp', 'tp')),
        P(None, None, ('dp', 'tp')),
        P(None, ('dp', 'tp'), None),
    )
    return jax.shard_map(body, mesh=mesh, in_specs=in_specs, out_specs=P('dp', None), check_vma=False)
```

profile of v0, /device:TPU:0, one launch (start us, length us, event | category | flops | bytes accessed | tf_op | source)
XLA Modules:
  0.0 533.5 jit_solution(16738521199234944806)
XLA Ops:
  6.5 1.4 slice_convert_fusion.1
  7.9 1.2 fusion.66
  9.1 9.3 %fusion.18 = bf16[128,4608]{1,0:T(8,128)(2,1)S(1)} fusion(bf16[2,2048,4608]{2,1,0:T(8,128)(2,1)} %param.15, bf16[128,2048]{1,0:T(8,128)(2,1)} %param.10, f32[2048]{0:T(1024)S(1)} %bitcast.87, f32[128]{0:T(128)S(1)} %add_rsqrt_fusion.3), kind=kOutput, calls=%fused_computation.20 | convolution fusion | flops 2417557504 | bytes 20587008 | tf_op jit(solution)/shard_map/dot_general | solution.py:26
  18.4 0.8 copy.13
  19.2 1.4 copy.14
  20.7 97.1 %slice_bitcast_fusion = (bf16[128,512,576]{1,2,0:T(8,128)(2,1)}, bf16[128,512,576]{1,2,0:T(8,128)(2,1)}) fusion(bf16[2,128,512,576]{2,3,1,0:T(8,128)(2,1)} %param.12), kind=kLoop, calls=%fused_computation.2 | loop fusion | bytes 301989888 | tf_op jit(solution)/shard_map/squeeze | solution.py:24
  117.8 25.5 %fusion.100 = (f32[128,8]{1,0:T(8,128)S(1)}, f32[128,8,512]{2,1,0:T(8,128)S(1)}) fusion(pred[128,512]{1,0:T(8,128)(4,1)S(1)} %iota_compare_fusion, bf16[128,8,576]{2,1,0:T(8,128)(2,1)S(1)} %copy.14, bf16[2,128,512,576]{2,3,1,0:T(8,128)(2,1)} %param.12), kind=kOutput, calls=%fused_computation.107 | convolution fusion | flops 606077440 | bytes 78843904 | tf_op jit(solution)/shard_map/sub | solution.py:28
  143.3 25.5 %fusion.56 = bf16[128,8,512]{2,1,0:T(8,128)(2,1)S(1)} fusion(bf16[128,512,576]{1,2,0:T(8,128)(2,1)} %get-tuple-element.12, f32[128,8,512]{2,1,0:T(8,128)S(1)} %get-tuple-element.18, f32[128,8]{1,0:T(8,128)S(1)} %get-tuple-element.17), kind=kOutput, calls=%fused_computation.52 | convolution fusion | flops 538443776 | bytes 70258688 | tf_op jit(solution)/shard_map/bht,btk->bhk/dot_general | solution.py:29
  168.8 0.4 copy.21
  169.2 7.1 %fusion.14 = f32[128,2048]{1,0:T(8,128)S(1)} fusion(bf16[128,4096]{1,0:T(8,128)(2,1)S(1)} %bitcast.82, bf16[2,4096,2048]{2,1,0:T(8,128)(2,1)} %param.16), kind=kOutput, calls=%fused_computation.16 | convolution fusion | flops 2147483648 | bytes 18874368 | tf_op jit(solution)/shard_map/dot_general | solution.py:31
  176.4 30.9 %all-reduce.4 = bf16[128,2048]{1,0:T(8,128)(2,1)S(1)} all-reduce(f32[128,2048]{1,0:T(8,128)S(1)} %fusion.14), channel_id=1, replica_groups=mesh['tp'=2,'dp'=4] {'tp'}, use_global_device_ids=true, to_apply=%region_3.4 | all-reduce | flops 262144 | bytes 1572864 | tf_op jit(solution)/shard_map/psum | solution.py:31
  207.7 1.0 fusion.71
  208.9 19.5 %all-gather.3.cloned.1.call-done = bf16[512,2048]{1,0:T(8,128)(2,1)} async-done(((bf16[128,2048]{1,0:T(8,128)(2,1)}), bf16[512,2048]{1,0:T(8,128)(2,1)}) %all-gather.3.cloned.1.call-update) | async-done | bytes 2097168 | tf_op jit(solution)/shard_map/all_gather | solution.py:34
  228.4 8.5 %fusion.34 = f32[512,1408]{1,0:T(8,128)} fusion(bf16[512,2048]{1,0:T(8,128)(2,1)} %all-gather.3.cloned.1.call-done, bf16[2,2048,1408]{2,1,0:T(8,128)(2,1)} %param.18), kind=kOutput, calls=%fused_computation.32 | convolution fusion | flops 2952790016 | bytes 10747904 | tf_op jit(solution)/shard_map/dot_general | solution.py:35
  236.9 13.9 %fusion.30 = f32[512,2048]{1,0:T(8,128)} fusion(bf16[2,1408,2048]{2,1,0:T(8,128)(2,1)} %param.19, bf16[512,2048]{1,0:T(8,128)(2,1)S(1)} %copy-done.6, bf16[2,2048,1408]{2,1,0:T(8,128)(2,1)} %param.17, f32[512,1408]{1,0:T(8,128)} %fusion.34), kind=kOutput, calls=%fused_computation.28 | convolution fusion | flops 5909905408 | bytes 20709376 | tf_op jit(solution)/shard_map/dot_general | solution.py:38
  250.8 38.4 %reduce-scatter.3.cloned.1.call-done = f32[128,2048]{1,0:T(8,128)} async-done(((f32[512,2048]{1,0:T(8,128)}), f32[128,2048]{1,0:T(8,128)}) %reduce-scatter.3.cloned.1.call-update) | async-done | bytes 1048592 | tf_op jit(solution)/shard_map/reduce_scatter | solution.py:39
  289.2 29.4 %all-reduce.5 = bf16[128,2048]{1,0:T(8,128)(2,1)S(1)} all-reduce(f32[128,2048]{1,0:T(8,128)} %reduce-scatter.3.cloned.1.call-done), channel_id=1, replica_groups=mesh['tp'=2,'dp'=4] {'tp'}, use_global_device_ids=true, to_apply=%region_6.7 | all-reduce | flops 262144 | bytes 1572864 | tf_op jit(solution)/shard_map/psum | solution.py:40
  318.9 0.8 copy-done.1
  319.7 9.1 %fusion.21 = bf16[128,4608]{1,0:T(8,128)(2,1)S(1)} fusion(bf16[2,2048,4608]{2,1,0:T(8,128)(2,1)} %param.15, bf16[128,2048]{1,0:T(8,128)(2,1)S(1)} %get-tuple-element.8, f32[2048]{0:T(1024)S(1)} %bitcast.86, f32[128]{0:T(128)S(1)} %add_rsqrt_fusion.1), kind=kOutput, calls=%fused_computation.21 | convolution fusion | flops 2417557504 | bytes 20587008 | tf_op jit(solution)/shard_map/dot_general | solution.py:26
  328.8 0.7 copy.16
  329.5 1.4 copy.17
  330.9 25.5 %fusion.101 = (f32[128,8]{1,0:T(8,128)S(1)}, f32[128,8,512]{2,1,0:T(8,128)S(1)}) fusion(pred[128,512]{1,0:T(8,128)(4,1)S(1)} %iota_compare_fusion, bf16[128,8,576]{2,1,0:T(8,128)(2,1)S(1)} %copy.17, bf16[2,128,512,576]{2,3,1,0:T(8,128)(2,1)} %param.12), kind=kOutput, calls=%fused_computation.108 | convolution fusion | flops 606077440 | bytes 78843904 | tf_op jit(solution)/shard_map/sub | solution.py:28
  356.4 25.5 %fusion.59 = bf16[128,8,512]{2,1,0:T(8,128)(2,1)S(1)} fusion(bf16[128,512,576]{1,2,0:T(8,128)(2,1)} %get-tuple-element.11, f32[128,8,512]{2,1,0:T(8,128)S(1)} %get-tuple-element.20, f32[128,8]{1,0:T(8,128)S(1)} %get-tuple-element.19), kind=kOutput, calls=%fused_computation.53 | convolution fusion | flops 538443776 | bytes 70258688 | tf_op jit(solution)/shard_map/bht,btk->bhk/dot_general | solution.py:29
  382.3 7.1 %fusion.12 = f32[128,2048]{1,0:T(8,128)S(1)} fusion(bf16[128,4096]{1,0:T(8,128)(2,1)S(1)} %bitcast.83, bf16[2,4096,2048]{2,1,0:T(8,128)(2,1)} %param.16), kind=kOutput, calls=%fused_computation.14 | convolution fusion | flops 2147483648 | bytes 18874368 | tf_op jit(solution)/shard_map/dot_general | solution.py:31
  389.5 26.0 %all-reduce.6 = bf16[128,2048]{1,0:T(8,128)(2,1)S(1)} all-reduce(f32[128,2048]{1,0:T(8,128)S(1)} %fusion.12), channel_id=1, replica_groups=mesh['tp'=2,'dp'=4] {'tp'}, use_global_device_ids=true, to_apply=%region_10.11 | all-reduce | flops 262144 | bytes 1572864 | tf_op jit(solution)/shard_map/psum | solution.py:31
  415.8 1.0 fusion.77
  417.2 19.0 %all-gather.5.cloned.1.call-done = bf16[512,2048]{1,0:T(8,128)(2,1)} async-done(((bf16[128,2048]{1,0:T(8,128)(2,1)}), bf16[512,2048]{1,0:T(8,128)(2,1)}) %all-gather.5.cloned.1.call-update) | async-done | bytes 2097168 | tf_op jit(solution)/shard_map/all_gather | solution.py:34
  436.2 8.4 %fusion.28 = f32[512,1408]{1,0:T(8,128)} fusion(bf16[512,2048]{1,0:T(8,128)(2,1)} %all-gather.5.cloned.1.call-done, bf16[2,2048,1408]{2,1,0:T(8,128)(2,1)} %param.18), kind=kOutput, calls=%fused_computation.26 | convolution fusion | flops 2952790016 | bytes 10747904 | tf_op jit(solution)/shard_map/dot_general | solution.py:35
  444.6 13.9 %fusion.24 = f32[512,2048]{1,0:T(8,128)} fusion(bf16[2,1408,2048]{2,1,0:T(8,128)(2,1)} %param.19, bf16[512,2048]{1,0:T(8,128)(2,1)S(1)} %copy-done.7, bf16[2,2048,1408]{2,1,0:T(8,128)(2,1)} %param.17, f32[512,1408]{1,0:T(8,128)} %fusion.28), kind=kOutput, calls=%fused_computation.22 | convolution fusion | flops 5909905408 | bytes 20709376 | tf_op jit(solution)/shard_map/dot_general | solution.py:38
  458.5 38.4 %reduce-scatter.5.cloned.1.call-done = f32[128,2048]{1,0:T(8,128)} async-done(((f32[512,2048]{1,0:T(8,128)}), f32[128,2048]{1,0:T(8,128)}) %reduce-scatter.5.cloned.1.call-update) | async-done | bytes 1048592 | tf_op jit(solution)/shard_map/reduce_scatter | solution.py:39
  496.9 29.2 %all-reduce.7 = bf16[128,2048]{1,0:T(8,128)(2,1)S(1)} all-reduce(f32[128,2048]{1,0:T(8,128)} %reduce-scatter.5.cloned.1.call-done), channel_id=1, replica_groups=mesh['tp'=2,'dp'=4] {'tp'}, use_global_device_ids=true, to_apply=%region_13.14 | all-reduce | flops 262144 | bytes 1572864 | tf_op jit(solution)/shard_map/psum | solution.py:40
  526.1 0.9 add.87
  (33 shorter events, 2.1 us)
Async XLA Ops:
  6.5 221.9 %all-gather.3.cloned.1.call-start = ((), (), s32[]{:S(2)}) async-start(), calls=%async_computation.2 | async-start | bytes 2621440 | tf_op jit(solution)/shard_map/all_gather | solution.py:34
  18.4 2.2 copy-start.5
  169.2 38.1 %copy-start = (bf16[128,2048]{1,0:T(8,128)(2,1)S(1)}, bf16[128,2048]{1,0:T(8,128)(2,1)}, u32[]{:S(2)}) copy-start(bf16[128,2048]{1,0:T(8,128)(2,1)} %param.10) | copy-start | bytes 1572868
  176.4 31.3 %copy-start.3 = (bf16[2,2048]{1,0:T(2,128)(2,1)S(1)}, bf16[2,2048]{1,0:T(2,128)(2,1)}, u32[]{:S(2)}) copy-start(bf16[2,2048]{1,0:T(2,128)(2,1)} %param.14) | copy-start | bytes 24580
  208.7 80.5 %reduce-scatter.3.cloned.1.call-start = ((), (), s32[]{:S(2)}) async-start(), calls=%async_computation.3 | async-start | bytes 5242880 | tf_op jit(solution)/shard_map/reduce_scatter | solution.py:39
  228.4 8.5 %copy-start.6 = (bf16[512,2048]{1,0:T(8,128)(2,1)S(1)}, bf16[512,2048]{1,0:T(8,128)(2,1)}, u32[]{:S(2)}) copy-start(bf16[512,2048]{1,0:T(8,128)(2,1)} %all-gather.3.cloned.1.call-done) | copy-start | bytes 6291460
  250.8 68.9 %copy-start.4 = (f32[1,2048]{1,0:T(1,128)S(1)}, f32[1,2048]{1,0:T(1,128)}, u32[]{:S(2)}) copy-start(f32[1,2048]{1,0:T(1,128)} %get-tuple-element.15) | copy-start | bytes 24580
  250.8 185.4 %all-gather.5.cloned.1.call-start = ((), (), s32[]{:S(2)}) async-start(), calls=%async_computation.4 | async-start | bytes 2621440 | tf_op jit(solution)/shard_map/all_gather | solution.py:34
  318.9 0.8 copy-start.1
  382.3 33.2 %copy-start.2 = (bf16[128,2048]{1,0:T(8,128)(2,1)S(1)}, bf16[128,2048]{1,0:T(8,128)(2,1)}, u32[]{:S(2)}) copy-start(bf16[128,2048]{1,0:T(8,128)(2,1)} %copy-done.1) | copy-start | bytes 1572868
  416.9 80.1 %reduce-scatter.5.cloned.1.call-start = ((), (), s32[]{:S(2)}) async-start(), calls=%async_computation.5 | async-start | bytes 5242880 | tf_op jit(solution)/shard_map/reduce_scatter | solution.py:39
  436.2 8.4 %copy-start.7 = (bf16[512,2048]{1,0:T(8,128)(2,1)S(1)}, bf16[512,2048]{1,0:T(8,128)(2,1)}, u32[]{:S(2)}) copy-start(bf16[512,2048]{1,0:T(8,128)(2,1)} %all-gather.5.cloned.1.call-done) | copy-start | bytes 6291460
Sparse Core Ops, SparseCore 0:
  208.8 19.5 all-gather.2
  250.9 38.2 reduce-scatter.2
  417.0 19.1 all-gather.4
  458.6 38.2 reduce-scatter.4
where the time goes:
time: 534 us
  matrix products  179 us (34%)
  blocking collectives  116 us (22%)
  waiting for transfers between devices  115 us (22%)
  local copies, waits for them, and re-layouts  103 us (19%)
  between operations  13.4 us (3%)
  other arithmetic  6.49 us (1%)
    squeeze x1, local copies, waits for them, and re-layouts, body(): c = cache[l]  97.1 us
    reduce_scatter x2, waiting for transfers between devices, body(): y = lax.psum_scatter(yp, 'dp', scatter_dimension=0, tiled=True)  76.8 us
    psum x2, blocking collectives, body(): y = lax.psum(y, 'tp')  58.5 us
    psum x2, blocking collectives, body(): attn = lax.psum(jnp.dot(o, wo[l], preferred_element_type=jnp.float32), 'tp')  57 us
    sub x2, matrix products, body(): jax.nn.softmax(jnp.where(keep, s, -jnp.inf), axis=-1).astype(jnp.bfloat16)  51 us
    dot_general x2, matrix products, body(): jnp.einsum('bht,btk->bhk', p, c[:, :, :LAT], preferred_element_type=jnp.f...  51 us
    all_gather x2, waiting for transfers between devices, body(): gg = lax.all_gather(g, 'dp', axis=0, tiled=True)  38.5 us
    dot_general x2, matrix products, body(): yp = jnp.dot(a, w2[l], preferred_element_type=jnp.float32)  27.7 us
  transfers between devices with their start and end apart: 4, of which 4 were waited for; matrix products, arithmetic and copies ran while one was open for 0% of the time, Pallas kernels for 0%

commit v1 on v0

v1 whole, which is shorter than its diff:
```python
import functools

import jax
import jax.numpy as jnp
from jax import lax
from jax.experimental import pallas as pl
from jax.experimental.pallas import tpu as pltpu
from jax.sharding import PartitionSpec as P

LAT = 512
EPS = 1e-6
SCALE = 192 ** -0.5
BF = jnp.bfloat16
F32 = jnp.float32


def _rmsnorm(v, w):
    vf = v.astype(F32)
    r = lax.rsqrt(jnp.mean(vf * vf, axis=-1, keepdims=True) + EPS)
    return (vf * r * w.astype(F32)).astype(BF)


def _attn_kernel(layer, G, NS, order_ref, lens_ref, q_ref, ct_ref, o_ref, buf, sems):
    nb, nh, _ = q_ref.shape
    nmax = ct_ref.shape[3] // 128
    ng = nb // G

    def chunks(g):
        return lax.div(lens_ref[order_ref[g * G + G - 1]] + 127, 128)

    def copies(g, n):
        slot = lax.rem(g, NS)
        return [pltpu.make_async_copy(
            ct_ref.at[layer, order_ref[g * G + s], :, pl.ds(0, n * 128)],
            buf.at[slot, s, :, pl.ds(0, n * 128)],
            sems.at[slot, s]) for s in range(G)]

    def start(g):
        c = chunks(g)
        for n in range(1, nmax + 1):
            @pl.when(c == n)
            def _():
                for cp in copies(g, n):
                    cp.start()

    for g in range(NS - 1):
        start(g)

    def body(g, carry):
        @pl.when(g + NS - 1 < ng)
        def _():
            start(g + NS - 1)
        c = chunks(g)
        slot = lax.rem(g, NS)
        for n in range(1, nmax + 1):
            @pl.when(c == n)
            def _():
                N = n * 128
                for cp in copies(g, n):
                    cp.wait()
                bs = [order_ref[g * G + s] for s in range(G)]
                scs = [jnp.dot(q_ref[bs[s]], buf[slot, s, :, 0:N], preferred_element_type=F32)
                       for s in range(G)]
                pos = lax.broadcasted_iota(jnp.int32, (nh, N), 1)
                scs = [jnp.where(pos < lens_ref[bs[s]], scs[s] * SCALE, -jnp.inf) for s in range(G)]
                ms = [jnp.max(sc, axis=-1, keepdims=True) for sc in scs]
                es = [jnp.exp(sc - m) for sc, m in zip(scs, ms)]
                ds = [jnp.sum(e, axis=-1, keepdims=True) for e in es]
                ps = [(e / d).astype(BF) for e, d in zip(es, ds)]
                outs = [lax.dot_general(ps[s], buf[slot, s, 0:LAT, 0:N], (((1,), (1,)), ((), ())),
                                        preferred_element_type=F32) for s in range(G)]
                for s in range(G):
                    o_ref[bs[s]] = outs[s].astype(BF)
        return carry

    lax.fori_loop(0, ng, body, 0)


def _attention(layer, q, ct, order, lens, G=8, NS=3):
    nb, nh, kv = q.shape
    s_len = ct.shape[3]
    smem = pl.BlockSpec(memory_space=pltpu.SMEM)
    vmem = pl.BlockSpec(memory_space=pltpu.VMEM)
    return pl.pallas_call(
        functools.partial(_attn_kernel, layer, G, NS),
        out_shape=jax.ShapeDtypeStruct((nb, nh, LAT), BF),
        in_specs=[smem, smem, vmem, pl.BlockSpec(memory_space=pl.ANY)],
        out_specs=vmem,
        scratch_shapes=[pltpu.VMEM((NS, G, kv, s_len), BF), pltpu.SemaphoreType.DMA((NS, G))],
        compiler_params=pltpu.CompilerParams(vmem_limit_bytes=48 * 2 ** 20),
        name=f"attn{layer}",
    )(order, lens, q, ct)


def _sort_order(lens):
    i = jnp.arange(lens.shape[0])
    before = (lens[None, :] < lens[:, None]) | ((lens[None, :] == lens[:, None]) & (i[None, :] < i[:, None]))
    rank = jnp.sum(before.astype(jnp.int32), axis=1)
    return jnp.sum(jnp.where(rank[:, None] == i[None, :], i[:, None], 0), axis=0).astype(jnp.int32)


def solution(mesh):
    def body(x, lengths, cache, attn_norm, ffn_norm, wq, wo, w1, w3, w2):
        nb = x.shape[0]
        n_layers, _, s_len, kv = cache.shape
        nh = wq.shape[2] // kv
        ct = jnp.swapaxes(cache, 2, 3)
        order = _sort_order(lengths)
        for l in range(n_layers):
            h = _rmsnorm(x, attn_norm[l])
            q = jnp.dot(h, wq[l], preferred_element_type=F32).astype(BF).reshape(nb, nh, kv)
            o = _attention(l, q, ct, order, lengths).reshape(nb, nh * LAT)
            attn = lax.psum(jnp.dot(o, wo[l], preferred_element_type=F32), 'tp')
            x = x + attn.astype(BF)
            g = _rmsnorm(x, ffn_norm[l])
            gg = lax.all_gather(g, 'dp', axis=0, tiled=True)
            u = jnp.dot(gg, w3[l], preferred_element_type=F32)
            v = jnp.dot(gg, w1[l], preferred_element_type=F32)
            a = (jax.nn.silu(u) * v).astype(BF)
            yp = jnp.dot(a, w2[l], preferred_element_type=F32)
            y = lax.psum_scatter(yp, 'dp', scatter_dimension=0, tiled=True)
            y = lax.psum(y, 'tp')
            x = x + y.astype(BF)
        return x

    in_specs = (
        P('dp', None),
        P('dp'),
        P(None, 'dp', None, None),
        P(None, None),
        P(None, None),
        P(None, None, 'tp'),
        P(None, 'tp', None),
        P(None, None, ('dp', 'tp')),
        P(None, None, ('dp', 'tp')),
        P(None, ('dp', 'tp'), None),
    )
    return jax.shard_map(body, mesh=mesh, in_specs=in_specs, out_specs=P('dp', None), check_vma=False)
```

time: 534 us -> 387 us (0.72)
  matrix products: 179 us -> 77.2 us
  local copies, waits for them, and re-layouts: 103 us -> 5.06 us
  Pallas kernels: 0 us -> 50.9 us
    squeeze x1 -> x0, local copies, waits for them, and re-layouts: 97.1 us -> none  [body(): c = cache[l]]
    dot_general x10 -> x8, matrix products: 128 us -> 77.2 us  [the longest x2 27.6 us: body(): yp = jnp.dot(a, w2[l], preferred_element_type=F32)]
    sub x2 -> x0, matrix products: 51 us -> none  [body(): jax.nn.softmax(jnp.where(keep, s, -jnp.inf), axis=-1).astype(jnp.bfloat16)]
    pallas_call x0 -> x2, Pallas kernels: none -> 50.9 us  [_attention(): pl.pallas_call(functools.partial(_attn_kernel, layer, G, NS), out_shape=j...]
where the time goes in v1:
time: 387 us
  blocking collectives  116 us (30%)
  waiting for transfers between devices  116 us (30%)
  matrix products  77.2 us (20%)
  Pallas kernels  50.9 us (13%)
  between operations  13.3 us (3%)
  other arithmetic  8.19 us (2%)
  local copies, waits for them, and re-layouts  5.06 us (1%)
    reduce_scatter x2, waiting for transfers between devices, body(): y = lax.psum_scatter(yp, 'dp', scatter_dimension=0, tiled=True)  76.8 us
    psum x2, blocking collectives, body(): y = lax.psum(y, 'tp')  58.5 us
    psum x2, blocking collectives, body(): attn = lax.psum(jnp.dot(o, wo[l], preferred_element_type=F32), 'tp')  58 us
    pallas_call x2, Pallas kernels, _attention(): pl.pallas_call(functools.partial(_attn_kernel, layer, G, NS), out_shape=j...  50.9 us
    all_gather x2, waiting for transfers between devices, body(): gg = lax.all_gather(g, 'dp', axis=0, tiled=True)  38.8 us
    dot_general x2, matrix products, body(): yp = jnp.dot(a, w2[l], preferred_element_type=F32)  27.6 us
    dot_general x2, matrix products, body(): jnp.dot(h, wq[l], preferred_element_type=F32).astype(BF).reshape(nb, nh, kv)  18.4 us
    dot_general x2, matrix products, body(): u = jnp.dot(gg, w3[l], preferred_element_type=F32)  16.9 us
  transfers between devices with their start and end apart: 4, of which 4 were waited for; matrix products, arithmetic and copies ran while one was open for 0% of the time, Pallas kernels for 0%

profile of v1, /device:TPU:0, one launch (start us, length us, event | category | flops | bytes accessed | tf_op | source)
XLA Modules:
  0.0 387.4 jit_solution(18344090955248745879)
XLA Ops:
  6.5 1.2 fusion.52
  7.8 0.9 convert_reduce_fusion
  8.8 0.8 slice_convert_fusion.1
  9.6 1.4 slice_convert_fusion
  11.0 9.3 %fusion.12 = bf16[128,4608]{1,0:T(8,128)(2,1)S(1)} fusion(bf16[2,2048,4608]{2,1,0:T(8,128)(2,1)} %param.15, bf16[128,2048]{1,0:T(8,128)(2,1)} %param.10, f32[2048]{0:T(1024)S(1)} %bitcast.72, f32[128]{0:T(128)S(1)} %add_rsqrt_fusion.3), kind=kOutput, calls=%fused_computation.12 | convolution fusion | flops 2417557504 | bytes 20587008 | tf_op jit(solution)/shard_map/dot_general | solution.py:111
  20.3 0.8 copy.15
  21.1 1.4 copy.16.q_ref
  22.4 25.4 %attn0.1 = bf16[128,8,512]{2,1,0:T(8,128)(2,1)S(1)} custom-call(s32[128]{0:T(128)S(1)} %select_reduce_fusion.order_ref, s32[128]{0:T(128)S(1)} %copy-done, bf16[128,8,576]{2,1,0:T(8,128)(2,1)S(1)} %copy.16.q_ref, bf16[2,128,576,512]{3,2,1,0:T(8,128)(2,1)} %bitcast.3.ct_ref), custom_call_target="tpu_custom_call" | custom-call | tf_op jit(solution)/shard_map/attn0/pallas_call | solution.py:84
  47.9 0.4 copy.19
  48.3 7.2 %fusion.8 = f32[128,2048]{1,0:T(8,128)S(1)} fusion(bf16[128,4096]{1,0:T(8,128)(2,1)S(1)} %bitcast.67, bf16[2,4096,2048]{2,1,0:T(8,128)(2,1)} %param.16), kind=kOutput, calls=%fused_computation.8 | convolution fusion | flops 2147483648 | bytes 18874368 | tf_op jit(solution)/shard_map/dot_general | solution.py:113
  55.4 31.6 %all-reduce.4 = bf16[128,2048]{1,0:T(8,128)(2,1)S(1)} all-reduce(f32[128,2048]{1,0:T(8,128)S(1)} %fusion.8), channel_id=1, replica_groups=mesh['tp'=2,'dp'=4] {'tp'}, use_global_device_ids=true, to_apply=%region_3.4 | all-reduce | flops 262144 | bytes 1572864 | tf_op jit(solution)/shard_map/psum | solution.py:113
  87.4 1.0 fusion.57
  88.6 19.9 %all-gather.3.cloned.1.call-done = bf16[512,2048]{1,0:T(8,128)(2,1)} async-done(((bf16[128,2048]{1,0:T(8,128)(2,1)}), bf16[512,2048]{1,0:T(8,128)(2,1)}) %all-gather.3.cloned.1.call-update) | async-done | bytes 2097168 | tf_op jit(solution)/shard_map/all_gather | solution.py:116
  108.6 8.4 %fusion.28 = f32[512,1408]{1,0:T(8,128)} fusion(bf16[512,2048]{1,0:T(8,128)(2,1)} %all-gather.3.cloned.1.call-done, bf16[2,2048,1408]{2,1,0:T(8,128)(2,1)} %param.18), kind=kOutput, calls=%fused_computation.24 | convolution fusion | flops 2952790016 | bytes 10747904 | tf_op jit(solution)/shard_map/dot_general | solution.py:117
  117.0 13.8 %fusion.24 = f32[512,2048]{1,0:T(8,128)} fusion(bf16[2,1408,2048]{2,1,0:T(8,128)(2,1)} %param.19, bf16[512,2048]{1,0:T(8,128)(2,1)S(1)} %copy-done.3, bf16[2,2048,1408]{2,1,0:T(8,128)(2,1)} %param.17, f32[512,1408]{1,0:T(8,128)} %fusion.28), kind=kOutput, calls=%fused_computation.20 | convolution fusion | flops 5909905408 | bytes 20709376 | tf_op jit(solution)/shard_map/dot_general | solution.py:120
  130.9 38.4 %reduce-scatter.3.cloned.1.call-done = f32[128,2048]{1,0:T(8,128)} async-done(((f32[512,2048]{1,0:T(8,128)}), f32[128,2048]{1,0:T(8,128)}) %reduce-scatter.3.cloned.1.call-update) | async-done | bytes 1048592 | tf_op jit(solution)/shard_map/reduce_scatter | solution.py:121
  169.3 29.3 %all-reduce.5 = bf16[128,2048]{1,0:T(8,128)(2,1)S(1)} all-reduce(f32[128,2048]{1,0:T(8,128)} %reduce-scatter.3.cloned.1.call-done), channel_id=1, replica_groups=mesh['tp'=2,'dp'=4] {'tp'}, use_global_device_ids=true, to_apply=%region_6.7 | all-reduce | flops 262144 | bytes 1572864 | tf_op jit(solution)/shard_map/psum | solution.py:122
  198.9 9.1 %fusion.15 = bf16[128,4608]{1,0:T(8,128)(2,1)S(1)} fusion(bf16[2,2048,4608]{2,1,0:T(8,128)(2,1)} %param.15, bf16[128,2048]{1,0:T(8,128)(2,1)S(1)} %get-tuple-element.8, f32[2048]{0:T(1024)S(1)} %bitcast.71, f32[128]{0:T(128)S(1)} %add_rsqrt_fusion.1), kind=kOutput, calls=%fused_computation.13 | convolution fusion | flops 2417557504 | bytes 20587008 | tf_op jit(solution)/shard_map/dot_general | solution.py:111
  208.0 0.7 copy.17
  208.7 1.4 copy.18.q_ref
  210.1 25.5 %attn1.1 = bf16[128,8,512]{2,1,0:T(8,128)(2,1)S(1)} custom-call(s32[128]{0:T(128)S(1)} %select_reduce_fusion.order_ref, s32[128]{0:T(128)S(1)} %copy-done, bf16[128,8,576]{2,1,0:T(8,128)(2,1)S(1)} %copy.18.q_ref, bf16[2,128,576,512]{3,2,1,0:T(8,128)(2,1)} %bitcast.3.ct_ref), custom_call_target="tpu_custom_call" | custom-call | tf_op jit(solution)/shard_map/attn1/pallas_call | solution.py:84
  235.6 0.4 copy.20
  236.0 7.1 %fusion.6 = f32[128,2048]{1,0:T(8,128)S(1)} fusion(bf16[128,4096]{1,0:T(8,128)(2,1)S(1)} %bitcast.68, bf16[2,4096,2048]{2,1,0:T(8,128)(2,1)} %param.16), kind=kOutput, calls=%fused_computation.6 | convolution fusion | flops 2147483648 | bytes 18874368 | tf_op jit(solution)/shard_map/dot_general | solution.py:113
  243.2 26.3 %all-reduce.6 = bf16[128,2048]{1,0:T(8,128)(2,1)S(1)} all-reduce(f32[128,2048]{1,0:T(8,128)S(1)} %fusion.6), channel_id=1, replica_groups=mesh['tp'=2,'dp'=4] {'tp'}, use_global_device_ids=true, to_apply=%region_8.9 | all-reduce | flops 262144 | bytes 1572864 | tf_op jit(solution)/shard_map/psum | solution.py:113
  269.8 1.0 fusion.63
  270.8 0.3 reduce-scatter.5.cloned.1.call-start
  271.1 18.9 %all-gather.5.cloned.1.call-done = bf16[512,2048]{1,0:T(8,128)(2,1)} async-done(((bf16[128,2048]{1,0:T(8,128)(2,1)}), bf16[512,2048]{1,0:T(8,128)(2,1)}) %all-gather.5.cloned.1.call-update) | async-done | bytes 2097168 | tf_op jit(solution)/shard_map/all_gather | solution.py:116
  290.0 8.4 %fusion.22 = f32[512,1408]{1,0:T(8,128)} fusion(bf16[512,2048]{1,0:T(8,128)(2,1)} %all-gather.5.cloned.1.call-done, bf16[2,2048,1408]{2,1,0:T(8,128)(2,1)} %param.18), kind=kOutput, calls=%fused_computation.18 | convolution fusion | flops 2952790016 | bytes 10747904 | tf_op jit(solution)/shard_map/dot_general | solution.py:117
  298.5 13.8 %fusion.18 = f32[512,2048]{1,0:T(8,128)} fusion(bf16[2,1408,2048]{2,1,0:T(8,128)(2,1)} %param.19, bf16[512,2048]{1,0:T(8,128)(2,1)S(1)} %copy-done.4, bf16[2,2048,1408]{2,1,0:T(8,128)(2,1)} %param.17, f32[512,1408]{1,0:T(8,128)} %fusion.22), kind=kOutput, calls=%fused_computation.14 | convolution fusion | flops 5909905408 | bytes 20709376 | tf_op jit(solution)/shard_map/dot_general | solution.py:120
  312.3 38.4 %reduce-scatter.5.cloned.1.call-done = f32[128,2048]{1,0:T(8,128)} async-done(((f32[512,2048]{1,0:T(8,128)}), f32[128,2048]{1,0:T(8,128)}) %reduce-scatter.5.cloned.1.call-update) | async-done | bytes 1048592 | tf_op jit(solution)/shard_map/reduce_scatter | solution.py:121
  350.7 29.1 %all-reduce.7 = bf16[128,2048]{1,0:T(8,128)(2,1)S(1)} all-reduce(f32[128,2048]{1,0:T(8,128)} %reduce-scatter.5.cloned.1.call-done), channel_id=1, replica_groups=mesh['tp'=2,'dp'=4] {'tp'}, use_global_device_ids=true, to_apply=%region_11.12 | all-reduce | flops 262144 | bytes 1572864 | tf_op jit(solution)/shard_map/psum | solution.py:122
  379.9 0.9 add.87
  (25 shorter events, 1.3 us)
Async XLA Ops:
  6.5 102.0 %all-gather.3.cloned.1.call-start = ((), (), s32[]{:S(2)}) async-start(), calls=%async_computation.2 | async-start | bytes 2621440 | tf_op jit(solution)/shard_map/all_gather | solution.py:116
  20.2 2.2 copy-start
  48.3 38.8 %copy-start.1 = (bf16[128,2048]{1,0:T(8,128)(2,1)S(1)}, bf16[128,2048]{1,0:T(8,128)(2,1)}, u32[]{:S(2)}) copy-start(bf16[128,2048]{1,0:T(8,128)(2,1)} %param.10) | copy-start | bytes 1572868
  88.4 80.8 %reduce-scatter.3.cloned.1.call-start = ((), (), s32[]{:S(2)}) async-start(), calls=%async_computation.3 | async-start | bytes 5242880 | tf_op jit(solution)/shard_map/reduce_scatter | solution.py:121
  108.6 8.4 %copy-start.3 = (bf16[512,2048]{1,0:T(8,128)(2,1)S(1)}, bf16[512,2048]{1,0:T(8,128)(2,1)}, u32[]{:S(2)}) copy-start(bf16[512,2048]{1,0:T(8,128)(2,1)} %all-gather.3.cloned.1.call-done) | copy-start | bytes 6291460
  130.8 159.2 %all-gather.5.cloned.1.call-start = ((), (), s32[]{:S(2)}) async-start(), calls=%async_computation.4 | async-start | bytes 2621440 | tf_op jit(solution)/shard_map/all_gather | solution.py:116
  243.2 26.7 %copy-start.2 = (f32[1,2048]{1,0:T(1,128)S(1)}, f32[1,2048]{1,0:T(1,128)}, u32[]{:S(2)}) copy-start(f32[1,2048]{1,0:T(1,128)} %get-tuple-element.11) | copy-start | bytes 24580
  270.8 79.9 %reduce-scatter.5.cloned.1.call-start = ((), (), s32[]{:S(2)}) async-start(), calls=%async_computation.5 | async-start | bytes 5242880 | tf_op jit(solution)/shard_map/reduce_scatter | solution.py:121
  290.0 8.4 %copy-start.4 = (bf16[512,2048]{1,0:T(8,128)(2,1)S(1)}, bf16[512,2048]{1,0:T(8,128)(2,1)}, u32[]{:S(2)}) copy-start(bf16[512,2048]{1,0:T(8,128)(2,1)} %all-gather.5.cloned.1.call-done) | copy-start | bytes 6291460
Sparse Core Ops, SparseCore 0:
  88.5 19.9 all-gather.2
  131.0 38.2 reduce-scatter.2
  270.9 19.0 all-gather.4
  312.5 38.2 reduce-scatter.4

commit v2 on v1

v2 whole, which is shorter than its diff:
```python
import functools

import jax
import jax.numpy as jnp
from jax import lax
from jax.experimental import pallas as pl
from jax.experimental.pallas import tpu as pltpu
from jax.sharding import PartitionSpec as P

LAT = 512
EPS = 1e-6
SCALE = 192 ** -0.5
BF = jnp.bfloat16
F32 = jnp.float32
MESH = pl.DeviceIdType.MESH
VMEM = pl.BlockSpec(memory_space=pltpu.VMEM)
SMEM = pl.BlockSpec(memory_space=pltpu.SMEM)
ANY = pl.BlockSpec(memory_space=pl.ANY)


def _rmsnorm(v, w):
    vf = v.astype(F32)
    r = lax.rsqrt(jnp.mean(vf * vf, axis=-1, keepdims=True) + EPS)
    return (vf * r * w.astype(F32)).astype(BF)


def _attn_kernel(layer, G, NS, order_ref, lens_ref, base_ref, q_ref, ct_ref, wo_ref, out_ref,
                 buf, sems, wbuf, wsems, o_s, oflat):
    nh = q_ref.shape[1]
    nmax = ct_ref.shape[3] // 128
    nb = order_ref.shape[0]
    ng = nb // G
    wrows = wbuf.shape[0] // ng

    def chunks(g):
        return lax.div(lens_ref[order_ref[g * G + G - 1]] + 127, 128)

    def copies(g, n):
        slot = lax.rem(g, NS)
        return [pltpu.make_async_copy(
            ct_ref.at[layer, order_ref[g * G + s], :, pl.ds(0, n * 128)],
            buf.at[slot, s, :, pl.ds(0, n * 128)],
            sems.at[slot, s]) for s in range(G)]

    def wcopy(g):
        rows = pl.ds(pl.multiple_of(g * wrows, wrows), wrows)
        return pltpu.make_async_copy(wo_ref.at[layer, rows, :], wbuf.at[rows, :], wsems.at[g])

    def start(g):
        c = chunks(g)
        for n in range(1, nmax + 1):
            @pl.when(c == n)
            def _():
                for cp in copies(g, n):
                    cp.start()

    for g in range(NS - 1):
        start(g)

    def body(g, carry):
        @pl.when(g + NS - 1 < ng)
        def _():
            start(g + NS - 1)
        wcopy(g).start()
        c = chunks(g)
        slot = lax.rem(g, NS)
        for n in range(1, nmax + 1):
            @pl.when(c == n)
            def _():
                N = n * 128
                for cp in copies(g, n):
                    cp.wait()
                bs = [order_ref[g * G + s] for s in range(G)]
                scs = [jnp.dot(q_ref[bs[s]], buf[slot, s, :, 0:N], preferred_element_type=F32)
                       for s in range(G)]
                pos = lax.broadcasted_iota(jnp.int32, (nh, N), 1)
                scs = [jnp.where(pos < lens_ref[bs[s]], scs[s] * SCALE, -jnp.inf) for s in range(G)]
                ms = [jnp.max(sc, axis=-1, keepdims=True) for sc in scs]
                es = [jnp.exp(sc - m) for sc, m in zip(scs, ms)]
                ds = [jnp.sum(e, axis=-1, keepdims=True) for e in es]
                ps = [(e / d).astype(BF) for e, d in zip(es, ds)]
                outs = [lax.dot_general(ps[s], buf[slot, s, 0:LAT, 0:N], (((1,), (1,)), ((), ())),
                                        preferred_element_type=F32) for s in range(G)]
                for s in range(G):
                    row = pl.multiple_of((bs[s] - base_ref[0]) * nh, nh)
                    for i in range(LAT // 128):
                        o_s[pl.ds(row + i * nb * nh, nh), :] = outs[s][:, i * 128:(i + 1) * 128]
        return carry

    lax.fori_loop(0, ng, body, 0)
    for h in range(nh):
        for i in range(LAT // 128):
            c = h * LAT + i * 128
            oflat[:, c:c + 128] = o_s[pl.ds(i * nb * nh + h, nb, stride=nh), :].astype(BF)
    for g in range(ng):
        wcopy(g).wait()
    nblk = 512

    def mm(j, carry):
        cols = pl.ds(pl.multiple_of(j * nblk, nblk), nblk)
        out_ref[:, cols] = jnp.dot(oflat[...], wbuf[:, cols], preferred_element_type=F32)
        return carry
    lax.fori_loop(0, out_ref.shape[1] // nblk, mm, 0)


def _attention(layer, q, ct, order, base, lens, wo, G=8, NS=3):
    _, nh, kv = q.shape
    nb = order.shape[0]
    s_len = ct.shape[3]
    hid, d = wo.shape[1], wo.shape[2]
    return pl.pallas_call(
        functools.partial(_attn_kernel, layer, G, NS),
        out_shape=jax.ShapeDtypeStruct((nb, d), F32),
        in_specs=[SMEM, SMEM, SMEM, VMEM, ANY, ANY],
        out_specs=VMEM,
        scratch_shapes=[
            pltpu.VMEM((NS, G, kv, s_len), BF), pltpu.SemaphoreType.DMA((NS, G)),
            pltpu.VMEM((hid, d), BF), pltpu.SemaphoreType.DMA((nb // G,)),
            pltpu.VMEM((LAT // 128 * nb * nh, 128), F32), pltpu.VMEM((nb, hid), BF),
        ],
        compiler_params=pltpu.CompilerParams(vmem_limit_bytes=48 * 2 ** 20),
        cost_estimate=pl.CostEstimate(flops=20 * 10 ** 9, bytes_accessed=40 * 2 ** 20, transcendentals=0),
        name=f"attn{layer}",
    )(order, lens, base, q, ct, wo)


def _sort_order(lens):
    i = jnp.arange(lens.shape[0])
    before = (lens[None, :] < lens[:, None]) | ((lens[None, :] == lens[:, None]) & (i[None, :] < i[:, None]))
    rank = jnp.sum(before.astype(jnp.int32), axis=1)
    return jnp.sum(jnp.where(rank[:, None] == i[None, :], i[:, None], 0), axis=0).astype(jnp.int32)


XLOC = {1: (1, 0), 0: (2, 0)}
YLOC = {0: (1, 1), 1: (2, 1)}


def _ffn_kernel(layer, last, CA, xo_ref, pa_ref, pb_ref, fn_ref, an_ref, w1_ref, w3_ref, w2_ref, wq_ref, *rest):
    if last:
        out_ref, rest = rest[0], rest[1:]
    else:
        xn_ref, q_ref, rest = rest[0], rest[1], rest[2:]
    (w13, w2v, wqv, gbuf, ybuf, sbuf, abuf, xp, xall,
     r1x_own, r1x_y, r1y_own, r1y_x, r2x, r2y,
     wsem, w2sem, wqsem, ss, rs) = rest
    tp = lax.axis_index("tp")
    dp = lax.axis_index("dp")
    xi, ci = lax.div(dp, 2), lax.rem(dp, 2)
    SIB = (tp, xi * 2 + 1 - ci)
    X = (tp, (1 - xi) * 2 + ci)
    Y = (1 - tp, dp)

    bar = pltpu.get_barrier_semaphore()
    for peer in (SIB, X, Y):
        pl.semaphore_signal(bar, inc=1, device_id=peer, device_id_type=MESH)

    nblk = w1_ref.shape[2] // 128
    wcopies = []
    for j in range(nblk):
        for i, w in enumerate((w3_ref, w1_ref)):
            wcopies.append(pltpu.make_async_copy(
                w.at[layer, :, pl.ds(j * 128, 128)], w13.at[:, pl.ds(j * 256 + i * 128, 128)],
                wsem.at[j, i]))
    w2copy = pltpu.make_async_copy(w2_ref.at[layer], w2v, w2sem)
    for cp in wcopies:
        cp.start()
    w2copy.start()
    wqcopies = []
    if not last:
        nq = wqsem.shape[0]
        qc = wqv.shape[1] // nq
        for j in range(nq):
            cols = pl.ds(j * qc, qc)
            wqcopies.append(pltpu.make_async_copy(wq_ref.at[layer + 1, :, cols], wqv.at[:, cols], wqsem.at[j]))
        for cp in wqcopies:
            cp.start()

    count = [0]

    def remote(src, dst, dev):
        i = count[0]
        count[0] += 1
        return pltpu.make_async_remote_copy(src_ref=src, dst_ref=dst, send_sem=ss.at[i], recv_sem=rs.at[i],
                                            device_id=dev, device_id_type=MESH)

    colA, colB = pl.ds(0, CA), pl.ds(CA, gbuf.shape[-1] - CA)
    own_sib = remote(gbuf.at[0, 0], gbuf.at[0, 1], SIB)
    own_x = {p: remote(gbuf.at[0, 0, p], gbuf.at[XLOC[p][0], 0, XLOC[p][1]], X) for p in (1, 0)}
    own_y = {p: remote(gbuf.at[0, 0, p], gbuf.at[YLOC[p][0], 0, YLOC[p][1]], Y) for p in (0, 1)}
    relay_x = remote(gbuf.at[1, 0, 1], gbuf.at[3, 0, 0], X)
    relay_y = remote(gbuf.at[1, 0, 0], gbuf.at[3, 0, 1], Y)
    sib_g = {k: remote(gbuf.at[k, 0], gbuf.at[k, 1], SIB) for k in (1, 2, 3)}
    sib_y = {k: remote(ybuf.at[k, 1], sbuf.at[k], SIB) for k in range(4)}
    st1_x = {p: remote(ybuf.at[XLOC[p][0], 0, XLOC[p][1], :, colA], r1x_own.at[p], X) for p in (0, 1)}
    st1_y = {p: remote(ybuf.at[YLOC[p][0], 0, YLOC[p][1], :, colB], r1y_own.at[p], Y) for p in (0, 1)}
    st1_dx = {p: remote(ybuf.at[3, 0, p, :, colA], r1x_y.at[p], X) for p in (0, 1)}
    st1_dy = {p: remote(ybuf.at[3, 0, p, :, colB], r1y_x.at[p], Y) for p in (0, 1)}
    st2_y = {p: remote(r1x_y.at[p], r2y.at[p], Y) for p in (0, 1)}
    st2_x = {p: remote(r1y_x.at[p], r2x.at[p], X) for p in (0, 1)}
    mine = [pl.ds(pl.multiple_of(tp * 64 + p * 32, 32), 32) for p in (0, 1)]
    xg = {p: remote(xall.at[mine[p]], xall.at[mine[p]], Y) for p in (0, 1)}

    x1 = xo_ref[...].astype(F32) + (pa_ref[...] + pb_ref[...]).astype(BF).astype(F32)
    x1 = x1.astype(BF)
    xp[...] = x1
    gbuf[0, 0] = _rmsnorm(x1, fn_ref[layer:layer + 1, :]).reshape(2, 32, -1)

    pl.semaphore_wait(bar, 3)
    own_sib.start()
    own_x[1].start()
    own_y[0].start()
    own_x[0].start()
    own_y[1].start()

    def combine(k):
        sib_y[k].wait_recv()
        ybuf[k, 0] = ybuf[k, 0] + sbuf[k]

    def chunk(k, carry):
        @pl.when(k == 0)
        def _():
            own_sib.wait_recv()
            for cp in wcopies:
                cp.wait()
        for kk in (1, 2, 3):
            @pl.when(k == kk)
            def _():
                sib_g[kk].wait_recv()
        g = gbuf[k].reshape(128, -1)
        for j in range(nblk):
            uv = jnp.dot(g, w13[:, j * 256:(j + 1) * 256], preferred_element_type=F32)
            u, v = uv[:, :128], uv[:, 128:]
            abuf[:, j * 128:(j + 1) * 128] = (jax.nn.silu(u) * v).astype(BF)

        @pl.when(k == 0)
        def _():
            own_x[1].wait_recv()
            own_y[0].wait_recv()
            relay_x.start()
            relay_y.start()
            sib_g[1].start()
            w2copy.wait()

        @pl.when(k == 1)
        def _():
            own_x[0].wait_recv()
            own_y[1].wait_recv()
            sib_g[2].start()
            combine(0)

        @pl.when(k == 2)
        def _():
            relay_x.wait_recv()
            relay_y.wait_recv()
            sib_g[3].start()
            combine(1)
            st1_x[1].start()
            st1_y[0].start()

        @pl.when(k == 3)
        def _():
            combine(2)
            st1_x[0].start()
            st1_y[1].start()

        a = abuf[...]
        nn = 512
        for j in range(ybuf.shape[-1] // nn):
            y = jnp.dot(a, w2v[:, j * nn:(j + 1) * nn], preferred_element_type=F32)
            ybuf[k, :, :, :, j * nn:(j + 1) * nn] = y.reshape(2, 2, 32, nn)
        for kk in range(4):
            @pl.when(k == kk)
            def _():
                sib_y[kk].start()
        return carry

    lax.fori_loop(0, 4, chunk, 0)
    sib_y[3].wait_recv()
    for p in (0, 1):
        ybuf[3, 0, p] = ybuf[3, 0, p] + sbuf[3, p]
        st1_dx[p].start()
        st1_dy[p].start()
    for p in (0, 1):
        st1_dx[p].wait_recv()
        k, j = YLOC[p]
        r1x_y[p] = r1x_y[p] + ybuf[k, 0, j, :, 0:CA]
        st2_y[p].start()
        st1_dy[p].wait_recv()
        k, j = XLOC[p]
        r1y_x[p] = r1y_x[p] + ybuf[k, 0, j, :, CA:]
        st2_x[p].start()
    for p in (0, 1):
        st1_x[p].wait_recv()
        st1_y[p].wait_recv()
        st2_y[p].wait_recv()
        st2_x[p].wait_recv()
        ya = ybuf[0, 0, p, :, 0:CA] + r1x_own[p] + r2y[p]
        yb = ybuf[0, 0, p, :, CA:] + r1y_own[p] + r2x[p]
        xv = xp[p * 32:(p + 1) * 32, :].astype(F32)
        y = jnp.concatenate([ya, yb], axis=-1).astype(BF).astype(F32)
        xn = (xv + y).astype(BF)
        xall[mine[p], :] = xn
        if not last:
            xn_ref[p * 32:(p + 1) * 32, :] = xn
        xg[p].start()
    for p in (0, 1):
        xg[p].wait_recv()
    if last:
        out_ref[...] = xall[...]
    else:
        h = _rmsnorm(xall[...], an_ref[layer + 1:layer + 2, :])
        for j, cp in enumerate(wqcopies):
            cp.wait()
            cols = pl.ds(j * qc, qc)
            q_ref[:, cols] = jnp.dot(h, wqv[:, cols], preferred_element_type=F32).astype(BF)
    for cp in [own_sib, relay_x, relay_y, *own_x.values(), *own_y.values(), *sib_g.values(), *sib_y.values(),
               *st1_x.values(), *st1_y.values(), *st1_dx.values(), *st1_dy.values(),
               *st2_x.values(), *st2_y.values(), *xg.values()]:
        cp.wait_send()


NCOPY = 31


def _ffn(layer, last, xo, pa, pb, fn, an, w1, w3, w2, wq, CA=1024):
    rows, d = xo.shape
    f = w1.shape[2]
    nq = wq.shape[2]
    nqs = 4
    if last:
        out_shape = [jax.ShapeDtypeStruct((2 * rows, d), BF)]
    else:
        out_shape = [jax.ShapeDtypeStruct((rows, d), BF), jax.ShapeDtypeStruct((2 * rows, nq), BF)]
    CB = d - CA
    scratch = [
        pltpu.VMEM((d, 2 * f), BF), pltpu.VMEM((f, d), BF),
        pltpu.VMEM((8, 128) if last else (d, nq), BF),
        pltpu.VMEM((4, 2, 2, 32, d), BF), pltpu.VMEM((4, 2, 2, 32, d), F32), pltpu.VMEM((4, 2, 32, d), F32),
        pltpu.VMEM((128, f), BF), pltpu.VMEM((rows, d), BF), pltpu.VMEM((2 * rows, d), BF),
        pltpu.VMEM((2, 32, CA), F32), pltpu.VMEM((2, 32, CA), F32),
        pltpu.VMEM((2, 32, CB), F32), pltpu.VMEM((2, 32, CB), F32),
        pltpu.VMEM((2, 32, CB), F32), pltpu.VMEM((2, 32, CA), F32),
        pltpu.SemaphoreType.DMA((f // 128, 2)), pltpu.SemaphoreType.DMA, pltpu.SemaphoreType.DMA((nqs,)),
        pltpu.SemaphoreType.DMA((NCOPY,)), pltpu.SemaphoreType.DMA((NCOPY,)),
    ]
    return pl.pallas_call(
        functools.partial(_ffn_kernel, layer, last, CA),
        out_shape=out_shape,
        in_specs=[VMEM, VMEM, VMEM, VMEM, VMEM, ANY, ANY, ANY, ANY],
        out_specs=[VMEM] * len(out_shape),
        scratch_shapes=scratch,
        compiler_params=pltpu.CompilerParams(collective_id=layer, has_side_effects=True,
                                             vmem_limit_bytes=62 * 2 ** 20),
        name=f"ffn{layer}",
    )(xo, pa, pb, fn, an, w1, w3, w2, wq)


def solution(mesh):
    def body(x, lengths, cache, attn_norm, ffn_norm, wq, wo, w1, w3, w2):
        nb = x.shape[0]
        n_layers, _, s_len, kv = cache.shape
        nh = wq.shape[2] // kv
        half = nb // 2
        tp = lax.axis_index('tp')
        ct = jnp.swapaxes(cache, 2, 3)
        ord0 = _sort_order(lengths[:half])
        ord1 = _sort_order(lengths[half:]) + half
        first = jnp.where(tp == 0, ord1, ord0)
        second = jnp.where(tp == 0, ord0, ord1)
        base1 = jnp.reshape((1 - tp) * half, (1,)).astype(jnp.int32)
        base2 = jnp.reshape(tp * half, (1,)).astype(jnp.int32)
        xo = lax.dynamic_slice_in_dim(x, tp * half, half, 0)
        h = _rmsnorm(x, attn_norm[0])
        q = jnp.dot(h, wq[0], preferred_element_type=F32).astype(BF)
        for l in range(n_layers):
            last = l == n_layers - 1
            q3 = q.reshape(nb, nh, kv)
            pa = _attention(l, q3, ct, first, base1, lengths, wo)
            pa = lax.ppermute(pa, 'tp', [(0, 1), (1, 0)])
            pb = _attention(l, q3, ct, second, base2, lengths, wo)
            res = _ffn(l, last, xo, pb, pa, ffn_norm, attn_norm, w1, w3, w2, wq)
            if last:
                return res[0]
            xo, q = res

    in_specs = (
        P('dp', None),
        P('dp'),
        P(None, 'dp', None, None),
        P(None, None),
        P(None, None),
        P(None, None, 'tp'),
        P(None, 'tp', None),
        P(None, None, ('dp', 'tp')),
        P(None, None, ('dp', 'tp')),
        P(None, ('dp', 'tp'), None),
    )
    return jax.shard_map(body, mesh=mesh, in_specs=in_specs, out_specs=P('dp', None), check_vma=False)
```

time: 387 us -> 193 us (0.50)
  Pallas kernels: 50.9 us -> 167 us
  blocking collectives: 116 us -> 0 us
  waiting for transfers between devices: 116 us -> 0.01 us
  matrix products: 77.2 us -> 9.27 us
  between operations: 13.3 us -> 0.15 us
  local copies, waits for them, and re-layouts: 5.06 us -> 11.9 us
  other arithmetic: 8.19 us -> 2.32 us
    psum x4 -> x0, blocking collectives: 116 us -> none  [the longest x2 58.5 us: body(): y = lax.psum(y, 'tp')]
    pallas_call x0 -> x2, Pallas kernels: none -> 94.1 us  [_ffn(): pl.pallas_call(functools.partial(_ffn_kernel, layer, last, CA), out_shape...]
    reduce_scatter x2 -> x0, waiting for transfers between devices: 76.8 us -> none  [body(): y = lax.psum_scatter(yp, 'dp', scatter_dimension=0, tiled=True)]
    dot_general x8 -> x1, matrix products: 77.2 us -> 9.27 us  [body(): q = jnp.dot(h, wq[0], preferred_element_type=F32).astype(BF)]
    all_gather x2 -> x0, waiting for transfers between devices: 38.8 us -> none  [body(): gg = lax.all_gather(g, 'dp', axis=0, tiled=True)]
    pallas_call x2 -> x4, Pallas kernels: 50.9 us -> 73.2 us  [_attention(): pl.pallas_call(functools.partial(_attn_kernel, layer, G, NS), out_shape=j...]
    unnamed x12 -> x13, local copies, waits for them, and re-layouts: 0.82 us -> 5.07 us
  transfers between devices with their start and end apart: 4 -> 2, of which waited for: 4 -> 0; matrix products, arithmetic and copies ran while one was open for 0% -> 0% of each run, Pallas kernels for 0% -> 18%
where the time goes in v2:
time: 193 us
  Pallas kernels  167 us (87%)
  local copies, waits for them, and re-layouts  11.9 us (6%)
  matrix products  9.27 us (5%)
  starting transfers between devices  2.46 us (1%)
  other arithmetic  2.32 us (1%)
    pallas_call x2, Pallas kernels, _ffn(): pl.pallas_call(functools.partial(_ffn_kernel, layer, last, CA), out_shape...  94.1 us
    pallas_call x4, Pallas kernels, _attention(): pl.pallas_call(functools.partial(_attn_kernel, layer, G, NS), out_shape=j...  73.2 us
    dot_general x1, matrix products, body(): q = jnp.dot(h, wq[0], preferred_element_type=F32).astype(BF)  9.27 us
    unnamed x13, local copies, waits for them, and re-layouts  5.07 us
  transfers between devices with their start and end apart: 2, of which 0 were waited for; matrix products, arithmetic and copies ran while one was open for 0% of the time, Pallas kernels for 18%

profile of v2, /device:TPU:0, one launch (start us, length us, event | category | flops | bytes accessed | tf_op | source)
XLA Modules:
  0.0 193.4 jit_solution(4260091982950243410)
XLA Ops:
  0.0 1.2 fusion.6
  1.2 0.8 fusion.16
  2.0 0.2 convert_reduce_fusion
  2.2 0.1 select_reduce_fusion
  2.3 0.1 select_reduce_fusion.1
  2.4 0.7 slice_convert_fusion
  3.1 0.0 copy-start.2
  3.1 9.3 %fusion.3 = bf16[128,4608]{1,0:T(8,128)(2,1)S(1)} fusion(bf16[2,2048,4608]{2,1,0:T(8,128)(2,1)} %wq_ref.3, bf16[128,2048]{1,0:T(8,128)(2,1)} %param.10, f32[2048]{0:T(1024)S(1)} %bitcast.13, f32[128]{0:T(128)S(1)} %add_rsqrt_fusion), kind=kOutput, calls=%fused_computation.3 | convolution fusion | flops 2417557504 | bytes 20587008 | tf_op jit(solution)/shard_map/dot_general | solution.py:374
  12.4 0.9 copy.17
  13.3 1.4 copy.18.q_ref
  14.7 0.0 copy-done.2
  14.7 18.7 %attn0.3 = f32[64,2048]{1,0:T(8,128)S(1)} custom-call(s32[64]{0:T(128)S(1)} %get-tuple-element.9.order_ref, s32[128]{0:T(128)S(1)} %copy-done.2, s32[1]{0:T(128)} %bitcast.5.base_ref, bf16[128,8,576]{2,1,0:T(8,128)(2,1)S(1)} %copy.18.q_ref, bf16[2,128,576,512]{3,2,1,0:T(8,128)(2,1)} %bitcast.4.ct_ref, bf16[2,4096,2048]{2,1,0:T(8,128)(2,1)} %wo_ref.7), custom_call_target="tpu_custom_call" | custom-call | flops 20000000000 | bytes 41943040 | tf_op jit(solution)/shard_map/attn0/pallas_call | solution.py:111
  33.4 2.4 %collective-permute-start = (f32[64,2048]{1,0:T(8,128)S(1)}, f32[64,2048]{1,0:T(8,128)S(1)}, u32[]{:S(2)}, u32[]{:S(2)}) collective-permute-start(f32[64,2048]{1,0:T(8,128)S(1)} %attn0.3), channel_id=1, source_target_pairs={{0,4},{4,0},{1,5},{5,1},{2,6},{6,2},{3,7},{7,3}} | collective-permute-start | bytes 1572872 | tf_op jit(solution)/shard_map/ppermute | solution.py:379
  35.9 17.7 %attn0.2.pa_ref = f32[64,2048]{1,0:T(8,128)S(1)} custom-call(s32[64]{0:T(128)S(1)} %get-tuple-element.10.order_ref, s32[128]{0:T(128)S(1)} %copy-done.2, s32[1]{0:T(128)} %bitcast.base_ref, bf16[128,8,576]{2,1,0:T(8,128)(2,1)S(1)} %copy.18.q_ref, bf16[2,128,576,512]{3,2,1,0:T(8,128)(2,1)} %bitcast.4.ct_ref, bf16[2,4096,2048]{2,1,0:T(8,128)(2,1)} %wo_ref.7), custom_call_target="tpu_custom_call" | custom-call | flops 20000000000 | bytes 41943040 | tf_op jit(solution)/shard_map/attn0/pallas_call | solution.py:111
  53.6 0.0 copy-start
  53.6 0.8 copy-done
  54.4 0.0 copy-done.3
  54.4 0.7 constant_dynamic-slice_fusion.xo_ref
  55.1 0.0 collective-permute-done.pb_ref
  55.1 0.8 copy-done.4
  56.0 50.3 %ffn0.1 = (bf16[64,2048]{1,0:T(8,128)(2,1)}, bf16[128,4608]{1,0:T(8,128)(2,1)}) custom-call(bf16[64,2048]{1,0:T(8,128)(2,1)} %constant_dynamic-slice_fusion.xo_ref, f32[64,2048]{1,0:T(8,128)} %copy-done, f32[64,2048]{1,0:T(8,128)} %copy-done.4, bf16[2,2048]{1,0:T(2,128)(2,1)} %fn_ref.3, bf16[2,2048]{1,0:T(2,128)(2,1)} %an_ref.3, ...), custom_call_target="tpu_custom_call" | custom-call | tf_op jit(solution)/shard_map/ffn0/pallas_call | solution.py:346
  106.3 1.7 copy.20
  108.0 1.4 copy.21.q_ref
  109.4 18.7 %attn1.3 = f32[64,2048]{1,0:T(8,128)S(1)} custom-call(s32[64]{0:T(128)S(1)} %get-tuple-element.9.order_ref, s32[128]{0:T(128)S(1)} %copy-done.2, s32[1]{0:T(128)} %bitcast.5.base_ref, bf16[128,8,576]{2,1,0:T(8,128)(2,1)S(1)} %copy.21.q_ref, bf16[2,128,576,512]{3,2,1,0:T(8,128)(2,1)} %bitcast.4.ct_ref, bf16[2,4096,2048]{2,1,0:T(8,128)(2,1)} %wo_ref.7), custom_call_target="tpu_custom_call" | custom-call | flops 20000000000 | bytes 41943040 | tf_op jit(solution)/shard_map/attn1/pallas_call | solution.py:111
  128.1 0.0 collective-permute-start.1
  128.2 18.0 %attn1.2.pa_ref = f32[64,2048]{1,0:T(8,128)S(1)} custom-call(s32[64]{0:T(128)S(1)} %get-tuple-element.10.order_ref, s32[128]{0:T(128)S(1)} %copy-done.2, s32[1]{0:T(128)} %bitcast.base_ref, bf16[128,8,576]{2,1,0:T(8,128)(2,1)S(1)} %copy.21.q_ref, bf16[2,128,576,512]{3,2,1,0:T(8,128)(2,1)} %bitcast.4.ct_ref, bf16[2,4096,2048]{2,1,0:T(8,128)(2,1)} %wo_ref.7), custom_call_target="tpu_custom_call" | custom-call | flops 20000000000 | bytes 41943040 | tf_op jit(solution)/shard_map/attn1/pallas_call | solution.py:111
  146.1 0.0 copy-start.1
  146.2 0.8 copy-done.1
  146.9 0.0 collective-permute-done.1.pb_ref
  146.9 0.8 copy-done.5
  147.7 43.7 %ffn1.1 = bf16[128,2048]{1,0:T(8,128)(2,1)} custom-call(bf16[64,2048]{1,0:T(8,128)(2,1)} %get-tuple-element.7.xo_ref, f32[64,2048]{1,0:T(8,128)} %copy-done.1, f32[64,2048]{1,0:T(8,128)} %copy-done.5, bf16[2,2048]{1,0:T(2,128)(2,1)} %fn_ref.3, bf16[2,2048]{1,0:T(2,128)(2,1)} %an_ref.3, bf16[2,2048,1408]{2,1,0:T(8,128)(2,1)} %w1_ref.3, ...), custom_call_target="tpu_custom_call" | custom-call | tf_op jit(solution)/shard_map/ffn1/pallas_call | solution.py:346
  191.5 1.9 copy.24
  (5 shorter events, 0.0 us)
Async XLA Ops:
  3.1 11.6 %copy-start.2 = (s32[128]{0:T(128)S(1)}, s32[128]{0:T(128)}, u32[]{:S(2)}) copy-start(s32[128]{0:T(128)} %lens_ref.7) | copy-start | bytes 1540
  33.4 21.7 %collective-permute-start = (f32[64,2048]{1,0:T(8,128)S(1)}, f32[64,2048]{1,0:T(8,128)S(1)}, u32[]{:S(2)}, u32[]{:S(2)}) collective-permute-start(f32[64,2048]{1,0:T(8,128)S(1)} %attn0.3), channel_id=1, source_target_pairs={{0,4},{4,0},{1,5},{5,1},{2,6},{6,2},{3,7},{7,3}} | collective-permute-start | bytes 1572872 | tf_op jit(solution)/shard_map/ppermute | solution.py:379
  35.9 18.5 %copy-start.3 = (bf16[128,2048]{1,0:T(8,128)(2,1)S(1)}, bf16[128,2048]{1,0:T(8,128)(2,1)}, u32[]{:S(2)}) copy-start(bf16[128,2048]{1,0:T(8,128)(2,1)} %param.10) | copy-start | bytes 1572868
  53.6 0.8 copy-start
  55.1 0.8 copy-start.4
  128.1 18.8 %collective-permute-start.1 = (f32[64,2048]{1,0:T(8,128)S(1)}, f32[64,2048]{1,0:T(8,128)S(1)}, u32[]{:S(2)}, u32[]{:S(2)}) collective-permute-start(f32[64,2048]{1,0:T(8,128)S(1)} %attn1.3), channel_id=1, source_target_pairs={{0,4},{4,0},{1,5},{5,1},{2,6},{6,2},{3,7},{7,3}} | collective-permute-start | bytes 1572872 | tf_op jit(solution)/shard_map/ppermute | solution.py:379
  146.1 0.8 copy-start.1
  146.9 0.8 copy-start.5

commit v3 on v2

v3 whole, which is shorter than its diff:
```python
import functools

import jax
import jax.numpy as jnp
from jax import lax
from jax.experimental import pallas as pl
from jax.experimental.pallas import tpu as pltpu
from jax.sharding import PartitionSpec as P

LAT = 512
EPS = 1e-6
SCALE = 192 ** -0.5
BF = jnp.bfloat16
F32 = jnp.float32
MESH = pl.DeviceIdType.MESH
VMEM = pl.BlockSpec(memory_space=pltpu.VMEM)
SMEM = pl.BlockSpec(memory_space=pltpu.SMEM)
ANY = pl.BlockSpec(memory_space=pl.ANY)


def _rmsnorm(v, w):
    vf = v.astype(F32)
    r = lax.rsqrt(jnp.mean(vf * vf, axis=-1, keepdims=True) + EPS)
    return (vf * r * w.astype(F32)).astype(BF)


def _project(h, w, j, q_ref, nb, nh, kv):
    nblk = -(-kv // 128)
    val = jnp.dot(h, w, preferred_element_type=F32).astype(BF).astype(F32)
    lo = (kv // 128) * 128
    odd = pltpu.roll(val[:, lo:lo + nblk * 128], nblk * 128 - (kv - lo), 1)
    for t, v in ((0, val), (1, odd)):
        for i in range(nblk):
            q_ref[pl.ds(i * nb * nh + 2 * j + t, nb, stride=nh), :] = v[:, i * 128:(i + 1) * 128]


def _first_kernel(lens_ref, x_ref, an_ref, wq_ref, order_ref, q_ref, wbuf, wsem):
    nb = x_ref.shape[0]
    kv2 = wbuf.shape[2]
    nj = wbuf.shape[0]
    cps = [pltpu.make_async_copy(wq_ref.at[0, :, pl.ds(j * kv2, kv2)], wbuf.at[j], wsem.at[j]) for j in range(nj)]
    for cp in cps:
        cp.start()
    tp = lax.axis_index("tp").astype(F32)
    half = nb // 2
    r = lax.broadcasted_iota(jnp.int32, (nb, nb), 0).astype(F32)
    c = lax.broadcasted_iota(jnp.int32, (nb, nb), 1).astype(F32)
    rh = (r >= half).astype(F32)
    ch = (c >= half).astype(F32)
    key = jnp.broadcast_to(lens_ref[...].astype(F32), (nb, nb)) * nb + c
    mine = jnp.sum(jnp.where(r == c, key, 0.0), axis=1, keepdims=True)
    rank = jnp.sum(jnp.where((rh == ch) & (key < mine), 1.0, 0.0), axis=1, keepdims=True)
    want = jnp.where(ch == 0.0, 1.0 - tp, tp)
    hit = (rank == c - ch * half) & (rh == want)
    order_ref[...] = jnp.sum(jnp.where(hit, r, 0.0), axis=0, keepdims=True).astype(jnp.int32)
    h = _rmsnorm(x_ref[...], an_ref[0:1, :])
    for j in range(nj):
        cps[j].wait()
        _project(h, wbuf[j], j, q_ref, nb, 2 * nj, kv2 // 2)


def _first(lens, x, an, wq, nh):
    nb, d = x.shape
    kv = wq.shape[2] // nh
    return pl.pallas_call(
        _first_kernel,
        out_shape=[jax.ShapeDtypeStruct((1, nb), jnp.int32),
                   jax.ShapeDtypeStruct((-(-kv // 128) * nb * nh, 128), F32)],
        in_specs=[VMEM, VMEM, VMEM, ANY],
        out_specs=[VMEM, VMEM],
        scratch_shapes=[pltpu.VMEM((nh // 2, d, 2 * kv), BF), pltpu.SemaphoreType.DMA((nh // 2,))],
        compiler_params=pltpu.CompilerParams(vmem_limit_bytes=32 * 2 ** 20),
        name="first",
    )(lens.reshape(1, nb), x, an, wq)


def _attn_kernel(layer, off, nh, G, NS, order_ref, lens_ref, q_ref, ct_ref, wo_ref, out_ref,
                 buf, sems, wbuf, wsems, o_s, oflat):
    kv = ct_ref.shape[2]
    nmax = ct_ref.shape[3] // 128
    nb = out_ref.shape[0]
    nall = ct_ref.shape[1]
    ng = nb // G
    wrows = wbuf.shape[0] // ng
    qblk = -(-kv // 128)

    def seq(i):
        return order_ref[0, off + i]

    def chunks(g):
        return lax.div(lens_ref[seq(g * G + G - 1)] + 127, 128)

    def copies(g, n):
        slot = lax.rem(g, NS)
        return [pltpu.make_async_copy(
            ct_ref.at[layer, seq(g * G + s), :, pl.ds(0, n * 128)],
            buf.at[slot, s, :, pl.ds(0, n * 128)],
            sems.at[slot, s]) for s in range(G)]

    def wcopy(g):
        rows = pl.ds(pl.multiple_of(g * wrows, wrows), wrows)
        return pltpu.make_async_copy(wo_ref.at[layer, rows, :], wbuf.at[rows, :], wsems.at[g])

    def start(g):
        c = chunks(g)
        for n in range(1, nmax + 1):
            @pl.when(c == n)
            def _():
                for cp in copies(g, n):
                    cp.start()

    def qrow(b):
        parts = [q_ref[pl.ds(pl.multiple_of(i * nall * nh + b * nh, nh), nh), :] for i in range(qblk)]
        return jnp.concatenate(parts, axis=-1)[:, :kv].astype(BF)

    for g in range(NS - 1):
        start(g)

    def body(g, carry):
        @pl.when(g + NS - 1 < ng)
        def _():
            start(g + NS - 1)
        wcopy(g).start()
        c = chunks(g)
        slot = lax.rem(g, NS)
        for n in range(1, nmax + 1):
            @pl.when(c == n)
            def _():
                N = n * 128
                for cp in copies(g, n):
                    cp.wait()
                bs = [seq(g * G + s) for s in range(G)]
                scs = [jnp.dot(qrow(bs[s]), buf[slot, s, :, 0:N], preferred_element_type=F32)
                       for s in range(G)]
                pos = lax.broadcasted_iota(jnp.int32, (nh, N), 1)
                scs = [jnp.where(pos < lens_ref[bs[s]], scs[s] * SCALE, -jnp.inf) for s in range(G)]
                ms = [jnp.max(sc, axis=-1, keepdims=True) for sc in scs]
                es = [jnp.exp(sc - m) for sc, m in zip(scs, ms)]
                ds = [jnp.sum(e, axis=-1, keepdims=True) for e in es]
                ps = [(e / d).astype(BF) for e, d in zip(es, ds)]
                outs = [lax.dot_general(ps[s], buf[slot, s, 0:LAT, 0:N], (((1,), (1,)), ((), ())),
                                        preferred_element_type=F32) for s in range(G)]
                for s in range(G):
                    row = lax.rem(bs[s], nb) * nh
                    for i in range(LAT // 128):
                        o_s[pl.ds(pl.multiple_of(row + i * nb * nh, nh), nh), :] = outs[s][:, i * 128:(i + 1) * 128]
        return carry

    lax.fori_loop(0, ng, body, 0)
    for h in range(nh):
        for i in range(LAT // 128):
            c = h * LAT + i * 128
            oflat[:, c:c + 128] = o_s[pl.ds(i * nb * nh + h, nb, stride=nh), :].astype(BF)
    for g in range(ng):
        wcopy(g).wait()
    nblk = 1024

    def mm(j, carry):
        cols = pl.ds(pl.multiple_of(j * nblk, nblk), nblk)
        out_ref[:, cols] = jnp.dot(oflat[...], wbuf[:, cols], preferred_element_type=F32)
        return carry
    lax.fori_loop(0, out_ref.shape[1] // nblk, mm, 0)


def _attention(layer, off, q, ct, order, lens, wo, nh, G=8, NS=3):
    kv, s_len = ct.shape[2:]
    nb = order.shape[1] // 2
    hid, d = wo.shape[1], wo.shape[2]
    return pl.pallas_call(
        functools.partial(_attn_kernel, layer, off, nh, G, NS),
        out_shape=jax.ShapeDtypeStruct((nb, d), F32),
        in_specs=[SMEM, SMEM, VMEM, ANY, ANY],
        out_specs=VMEM,
        scratch_shapes=[
            pltpu.VMEM((NS, G, kv, s_len), BF), pltpu.SemaphoreType.DMA((NS, G)),
            pltpu.VMEM((hid, d), BF), pltpu.SemaphoreType.DMA((nb // G,)),
            pltpu.VMEM((LAT // 128 * nb * nh, 128), F32), pltpu.VMEM((nb, hid), BF),
        ],
        compiler_params=pltpu.CompilerParams(vmem_limit_bytes=40 * 2 ** 20),
        cost_estimate=pl.CostEstimate(flops=20 * 10 ** 9, bytes_accessed=40 * 2 ** 20, transcendentals=0),
        name=f"attn{layer}",
    )(order, lens, q, ct, wo)


XLOC = {1: (1, 0), 0: (2, 0)}
YLOC = {0: (1, 1), 1: (2, 1)}
W = 512
A = (0, 1)
B = (2, 3)
QORDER = (0, 2, 1, 3)
HALF = 64


def _ffn_kernel(layer, last, nh, xo_ref, pa_ref, pb_ref, fn_ref, an_ref, w1_ref, w3_ref, w2_ref, wq_ref, *rest):
    if last:
        out_ref, rest = rest[0], rest[1:]
    else:
        xn_ref, q_ref, rest = rest[0], rest[1], rest[2:]
    (w13, w2v, wqv, gbuf, ybuf, sbuf, abuf, xp, xall,
     r1x_own, r1x_y, r1y_own, r1y_x, r2x, r2y,
     wsem, w2sem, wqsem, ss, rs) = rest
    tp = lax.axis_index("tp")
    dp = lax.axis_index("dp")
    xi, ci = lax.div(dp, 2), lax.rem(dp, 2)
    SIB = (tp, xi * 2 + 1 - ci)
    X = (tp, (1 - xi) * 2 + ci)
    Y = (1 - tp, dp)

    bar = pltpu.get_barrier_semaphore()
    for peer in (SIB, X, Y):
        pl.semaphore_signal(bar, inc=1, device_id=peer, device_id_type=MESH)

    nblk = w1_ref.shape[2] // 128
    wcopies = []
    for j in range(nblk):
        for i, w in enumerate((w3_ref, w1_ref)):
            wcopies.append(pltpu.make_async_copy(
                w.at[layer, :, pl.ds(j * 128, 128)], w13.at[:, pl.ds(j * 256 + i * 128, 128)],
                wsem.at[j, i]))
    w2copy = pltpu.make_async_copy(w2_ref.at[layer], w2v, w2sem)
    for cp in wcopies:
        cp.start()
    w2copy.start()
    nj = nh // 2
    if not last:
        kv2 = wq_ref.shape[2] // nj
        dst = [w13.at[:, pl.ds(j * kv2, kv2)] if j < 2 else wqv.at[j - 2] for j in range(nj)]
        wqcopies = [pltpu.make_async_copy(wq_ref.at[layer + 1, :, pl.ds(j * kv2, kv2)], dst[j], wqsem.at[j])
                    for j in range(nj)]
        for cp in wqcopies[2:]:
            cp.start()

    count = [16]

    def remote(src, dst, dev, i=None):
        if i is None:
            i = count[0]
            count[0] += 1
        return pltpu.make_async_remote_copy(src_ref=src, dst_ref=dst, send_sem=ss.at[i], recv_sem=rs.at[i],
                                            device_id=dev, device_id_type=MESH)

    def cols(q):
        return pl.ds(q * W, W)

    colA, colB = pl.ds(A[0] * W, len(A) * W), pl.ds(B[0] * W, len(B) * W)
    own_sib = remote(gbuf.at[0, 0], gbuf.at[0, 1], SIB)
    own_x = {p: remote(gbuf.at[0, 0, p], gbuf.at[XLOC[p][0], 0, XLOC[p][1]], X) for p in (1, 0)}
    own_y = {p: remote(gbuf.at[0, 0, p], gbuf.at[YLOC[p][0], 0, YLOC[p][1]], Y) for p in (0, 1)}
    relay_x = remote(gbuf.at[1, 0, 1], gbuf.at[3, 0, 0], X)
    relay_y = remote(gbuf.at[1, 0, 0], gbuf.at[3, 0, 1], Y)
    sib_g = {k: remote(gbuf.at[k, 0], gbuf.at[k, 1], SIB) for k in (1, 2, 3)}
    PS = (0, 1)
    st1_x = {p: remote(ybuf.at[XLOC[p][0], 0, XLOC[p][1], :, colA], r1x_own.at[p], X) for p in PS}
    st1_y = {p: remote(ybuf.at[YLOC[p][0], 0, YLOC[p][1], :, colB], r1y_own.at[p], Y) for p in PS}
    st1_dx = {(p, q): remote(ybuf.at[3, 0, p, :, cols(q)], r1x_y.at[p, i], X) for p in PS for i, q in enumerate(A)}
    st1_dy = {(p, q): remote(ybuf.at[3, 0, p, :, cols(q)], r1y_x.at[p, i], Y) for p in PS for i, q in enumerate(B)}
    st2_y = {(p, q): remote(r1x_y.at[p, i], r2y.at[p, i], Y) for p in PS for i, q in enumerate(A)}
    st2_x = {(p, q): remote(r1y_x.at[p, i], r2x.at[p, i], X) for p in PS for i, q in enumerate(B)}
    mine = [pl.ds(pl.multiple_of(tp * HALF + p * 32, 32), 32) for p in PS]
    xg = {(p, q): remote(xall.at[mine[p], cols(q)], xall.at[mine[p], cols(q)], Y) for p in PS for q in A + B}

    def sib_y(k, q):
        return remote(ybuf.at[k, 1, :, :, cols(q)], sbuf.at[k, :, :, cols(q)], SIB, k * 4 + q)

    if xo_ref.shape[0] == HALF:
        xo = xo_ref[...]
    else:
        xo = xo_ref[pl.ds(pl.multiple_of(tp * HALF, HALF), HALF), :]
    x1 = (xo.astype(F32) + (pa_ref[...] + pb_ref[...]).astype(BF).astype(F32)).astype(BF)
    xp[...] = x1
    gbuf[0, 0] = _rmsnorm(x1, fn_ref[layer:layer + 1, :]).reshape(2, 32, -1)

    pl.semaphore_wait(bar, 3)
    own_sib.start()
    own_x[1].start()
    own_y[0].start()
    own_x[0].start()
    own_y[1].start()

    def combine(k, q):
        sib_y(k, q).wait_recv()
        ybuf[k, 0, :, :, cols(q)] = ybuf[k, 0, :, :, cols(q)] + sbuf[k, :, :, cols(q)]

    def chunk(k, carry):
        @pl.when(k == 0)
        def _():
            own_sib.wait_recv()
            for cp in wcopies:
                cp.wait()
        for kk in (1, 2, 3):
            @pl.when(k == kk)
            def _():
                sib_g[kk].wait_recv()
        g = gbuf[k].reshape(2 * HALF, -1)
        for j in range(nblk):
            uv = jnp.dot(g, w13[:, j * 256:(j + 1) * 256], preferred_element_type=F32)
            u, v = uv[:, :128], uv[:, 128:]
            abuf[:, j * 128:(j + 1) * 128] = (jax.nn.silu(u) * v).astype(BF)

        @pl.when(k == 0)
        def _():
            own_x[1].wait_recv()
            own_y[0].wait_recv()
            relay_x.start()
            relay_y.start()
            sib_g[1].start()
            w2copy.wait()

        @pl.when(k == 1)
        def _():
            own_x[0].wait_recv()
            own_y[1].wait_recv()
            sib_g[2].start()
            for q in QORDER:
                combine(0, q)

        @pl.when(k == 2)
        def _():
            relay_x.wait_recv()
            relay_y.wait_recv()
            sib_g[3].start()
            for q in QORDER:
                combine(1, q)
            st1_x[1].start()
            st1_y[0].start()

        @pl.when(k == 3)
        def _():
            if not last:
                for cp in wqcopies[:2]:
                    cp.start()
            for q in QORDER:
                combine(2, q)
            st1_x[0].start()
            st1_y[1].start()

        a = abuf[...]
        for q in QORDER:
            y = jnp.dot(a, w2v[:, q * W:(q + 1) * W], preferred_element_type=F32)
            ybuf[k, :, :, :, q * W:(q + 1) * W] = y.reshape(2, 2, 32, W)
            sib_y(k, q).start()
        return carry

    lax.fori_loop(0, 4, chunk, 0)
    for q in QORDER:
        combine(3, q)
        for p in PS:
            (st1_dx if q in A else st1_dy)[p, q].start()
    for q in QORDER:
        for p in PS:
            if q in A:
                st1_dx[p, q].wait_recv()
                (k, j), i = YLOC[p], A.index(q)
                r1x_y[p, i] = r1x_y[p, i] + ybuf[k, 0, j, :, q * W:(q + 1) * W]
                st2_y[p, q].start()
            else:
                st1_dy[p, q].wait_recv()
                (k, j), i = XLOC[p], B.index(q)
                r1y_x[p, i] = r1y_x[p, i] + ybuf[k, 0, j, :, q * W:(q + 1) * W]
                st2_x[p, q].start()
    for p in PS:
        st1_x[p].wait_recv()
        st1_y[p].wait_recv()
    for q in QORDER:
        for p in PS:
            c = slice(q * W, (q + 1) * W)
            y = ybuf[0, 0, p, :, c]
            if q in A:
                st2_y[p, q].wait_recv()
                i = A.index(q)
                y = y + r1x_own[p, :, i * W:(i + 1) * W] + r2y[p, i]
            else:
                st2_x[p, q].wait_recv()
                i = B.index(q)
                y = y + r1y_own[p, :, i * W:(i + 1) * W] + r2x[p, i]
            xn = (xp[p * 32:(p + 1) * 32, c].astype(F32) + y.astype(BF).astype(F32)).astype(BF)
            xall[mine[p], c] = xn
            if not last:
                xn_ref[p * 32:(p + 1) * 32, c] = xn
            xg[p, q].start()
    for cp in xg.values():
        cp.wait_recv()
    if last:
        out_ref[...] = xall[...]
    else:
        h = _rmsnorm(xall[...], an_ref[layer + 1:layer + 2, :])
        for j, cp in enumerate(wqcopies):
            cp.wait()
            _project(h, dst[j][...], j, q_ref, 2 * HALF, nh, kv2 // 2)
    for cp in [own_sib, relay_x, relay_y, *own_x.values(), *own_y.values(), *sib_g.values(),
               *st1_x.values(), *st1_y.values(), *st1_dx.values(), *st1_dy.values(),
               *st2_x.values(), *st2_y.values(), *xg.values()]:
        cp.wait_send()
    for k in range(4):
        for q in QORDER:
            sib_y(k, q).wait_send()


NCOPY = 16 + 10 + 4 + 8 + 8 + 8


def _ffn(layer, last, nh, xo, pa, pb, fn, an, w1, w3, w2, wq):
    rows, d = pa.shape
    f = w1.shape[2]
    kv = wq.shape[2] // nh
    if last:
        out_shape = [jax.ShapeDtypeStruct((2 * rows, d), BF)]
    else:
        out_shape = [jax.ShapeDtypeStruct((rows, d), BF),
                     jax.ShapeDtypeStruct((-(-kv // 128) * 2 * rows * nh, 128), F32)]
    NA, NB = len(A), len(B)
    scratch = [
        pltpu.VMEM((d, 2 * f), BF), pltpu.VMEM((f, d), BF),
        pltpu.VMEM((1, 16, 128) if last else (nh // 2 - 2, d, 2 * kv), BF),
        pltpu.VMEM((4, 2, 2, 32, d), BF), pltpu.VMEM((4, 2, 2, 32, d), F32), pltpu.VMEM((4, 2, 32, d), F32),
        pltpu.VMEM((128, f), BF), pltpu.VMEM((rows, d), BF), pltpu.VMEM((2 * rows, d), BF),
        pltpu.VMEM((2, 32, NA * W), F32), pltpu.VMEM((2, NA, 32, W), F32),
        pltpu.VMEM((2, 32, NB * W), F32), pltpu.VMEM((2, NB, 32, W), F32),
        pltpu.VMEM((2, NB, 32, W), F32), pltpu.VMEM((2, NA, 32, W), F32),
        pltpu.SemaphoreType.DMA((f // 128, 2)), pltpu.SemaphoreType.DMA, pltpu.SemaphoreType.DMA((nh // 2,)),
        pltpu.SemaphoreType.DMA((NCOPY,)), pltpu.SemaphoreType.DMA((NCOPY,)),
    ]
    return pl.pallas_call(
        functools.partial(_ffn_kernel, layer, last, nh),
        out_shape=out_shape,
        in_specs=[VMEM, VMEM, VMEM, VMEM, VMEM, ANY, ANY, ANY, ANY],
        out_specs=[VMEM] * len(out_shape),
        scratch_shapes=scratch,
        compiler_params=pltpu.CompilerParams(collective_id=layer, has_side_effects=True,
                                             vmem_limit_bytes=46 * 2 ** 20),
        name=f"ffn{layer}",
    )(xo, pa, pb, fn, an, w1, w3, w2, wq)


def solution(mesh):
    def body(x, lengths, cache, attn_norm, ffn_norm, wq, wo, w1, w3, w2):
        nb = x.shape[0]
        n_layers, _, s_len, kv = cache.shape
        nh = wq.shape[2] // kv
        ct = jnp.swapaxes(cache, 2, 3)
        order, q = _first(lengths, x, attn_norm, wq, nh)
        for l in range(n_layers):
            last = l == n_layers - 1
            pa = _attention(l, 0, q, ct, order, lengths, wo, nh)
            pa = lax.ppermute(pa, 'tp', [(0, 1), (1, 0)])
            pb = _attention(l, nb // 2, q, ct, order, lengths, wo, nh)
            res = _ffn(l, last, nh, x, pb, pa, ffn_norm, attn_norm, w1, w3, w2, wq)
            if last:
                return res[0]
            x, q = res

    in_specs = (
        P('dp', None),
        P('dp'),
        P(None, 'dp', None, None),
        P(None, None),
        P(None, None),
        P(None, None, 'tp'),
        P(None, 'tp', None),
        P(None, None, ('dp', 'tp')),
        P(None, None, ('dp', 'tp')),
        P(None, ('dp', 'tp'), None),
    )
    return jax.shard_map(body, mesh=mesh, in_specs=in_specs, out_specs=P('dp', None), check_vma=False)
```

time: 193 us -> 176 us (0.912)
  matrix products: 9.27 us -> 0 us
  local copies, waits for them, and re-layouts: 11.9 us -> 3.21 us
  starting transfers between devices: 2.46 us -> 5.91 us
  other arithmetic: 2.32 us -> 0 us
    dot_general x1 -> x0, matrix products: 9.27 us -> none  [body(): q = jnp.dot(h, wq[0], preferred_element_type=F32).astype(BF)]
    ppermute x2, starting transfers between devices: 2.46 us -> 5.91 us  [body(): pa = lax.ppermute(pa, 'tp', [(0, 1), (1, 0)])]
    reshape x2 -> x0, local copies, waits for them, and re-layouts: 2.72 us -> none  [body(): q3 = q.reshape(nb, nh, kv)]
    unnamed x13 -> x15, local copies, waits for them, and re-layouts: 5.07 us -> 3.21 us
    pallas_call x6 -> x7, Pallas kernels: 167 us -> 167 us  [the longest x2 89.9 us: _ffn(): pl.pallas_call(functools.partial(_ffn_kernel, layer, last, nh), out_shape...]
  transfers between devices with their start and end apart: 2 -> 2, of which waited for: 0 -> 0; matrix products, arithmetic and copies ran while one was open for 0% -> 0% of each run, Pallas kernels for 18% -> 20%
where the time goes in v3:
time: 176 us; the launch traced here: 177 us
  Pallas kernels  167 us (95%)
  starting transfers between devices  5.91 us (3%)
  local copies, waits for them, and re-layouts  3.21 us (2%)
    pallas_call x2, Pallas kernels, _ffn(): pl.pallas_call(functools.partial(_ffn_kernel, layer, last, nh), out_shape...  89.9 us
    pallas_call x4, Pallas kernels, _attention(): pl.pallas_call(functools.partial(_attn_kernel, layer, off, nh, G, NS), ou...  70 us
    pallas_call x1, Pallas kernels, _first(): pl.pallas_call(_first_kernel, out_shape=[jax.ShapeDtypeStruct((1, nb), jn...  7.61 us
    ppermute x2, starting transfers between devices, body(): pa = lax.ppermute(pa, 'tp', [(0, 1), (1, 0)])  5.91 us
  transfers between devices with their start and end apart: 2, of which 0 were waited for; matrix products, arithmetic and copies ran while one was open for 0% of the time, Pallas kernels for 20%

profile of v3, /device:TPU:0, one launch (start us, length us, event | category | flops | bytes accessed | tf_op | source)
XLA Modules:
  0.0 176.7 jit_solution(7452874795996657712)
XLA Ops:
  0.0 0.0 copy-start
  0.0 1.0 copy-done
  1.0 0.0 copy-start.2
  1.0 0.7 copy-done.2
  1.7 0.0 copy-start.5
  1.7 0.7 copy-done.5
  2.4 0.0 copy-start.6
  2.4 7.6 %first.1 = (s32[1,128]{1,0:T(1,128)S(1)}, f32[5120,128]{1,0:T(8,128)S(1)}) custom-call(s32[1,128]{1,0:T(1,128)S(1)} %bitcast.2, bf16[128,2048]{1,0:T(8,128)(2,1)S(1)} %copy-done, bf16[2,2048]{1,0:T(2,128)(2,1)S(1)} %copy-done.2, bf16[2,2048,4608]{2,1,0:T(8,128)(2,1)} %wq_ref.5), custom_call_target="tpu_custom_call" | custom-call | tf_op jit(solution)/shard_map/first/pallas_call | solution.py:65
  10.0 0.0 copy-done.6
  10.0 17.4 %attn0.3 = f32[64,2048]{1,0:T(8,128)S(1)} custom-call(s32[1,128]{1,0:T(1,128)S(1)} %get-tuple-element.9.order_ref, s32[128]{0:T(128)S(1)} %copy-done.6, f32[5120,128]{1,0:T(8,128)S(1)} %get-tuple-element.10.q_ref, bf16[2,128,576,512]{3,2,1,0:T(8,128)(2,1)} %bitcast.1.ct_ref, bf16[2,4096,2048]{2,1,0:T(8,128)(2,1)} %wo_ref.7), custom_call_target="tpu_custom_call" | custom-call | flops 20000000000 | bytes 41943040 | tf_op jit(solution)/shard_map/attn0/pallas_call | solution.py:169
  27.5 0.0 copy-start.1
  27.5 0.0 copy-start.3
  27.5 0.0 copy-start.4
  27.5 3.4 %collective-permute-start = (f32[64,2048]{1,0:T(8,128)S(1)}, f32[64,2048]{1,0:T(8,128)S(1)}, u32[]{:S(2)}, u32[]{:S(2)}) collective-permute-start(f32[64,2048]{1,0:T(8,128)S(1)} %attn0.3), channel_id=1, source_target_pairs={{0,4},{4,0},{1,5},{5,1},{2,6},{6,2},{3,7},{7,3}} | collective-permute-start | bytes 1572872 | tf_op jit(solution)/shard_map/ppermute | solution.py:445
  30.9 17.4 %attn0.2.pa_ref = f32[64,2048]{1,0:T(8,128)S(1)} custom-call(s32[1,128]{1,0:T(1,128)S(1)} %get-tuple-element.9.order_ref, s32[128]{0:T(128)S(1)} %copy-done.6, f32[5120,128]{1,0:T(8,128)S(1)} %get-tuple-element.10.q_ref, bf16[2,128,576,512]{3,2,1,0:T(8,128)(2,1)} %bitcast.1.ct_ref, bf16[2,4096,2048]{2,1,0:T(8,128)(2,1)} %wo_ref.7), custom_call_target="tpu_custom_call" | custom-call | flops 20000000000 | bytes 41943040 | tf_op jit(solution)/shard_map/attn0/pallas_call | solution.py:169
  48.3 0.0 collective-permute-done.pb_ref
  48.3 0.0 copy-done.1
  48.3 0.0 copy-done.3
  48.4 0.0 copy-done.4
  48.4 47.6 %ffn0.1 = (bf16[64,2048]{1,0:T(8,128)(2,1)S(1)}, f32[5120,128]{1,0:T(8,128)S(1)}) custom-call(bf16[128,2048]{1,0:T(8,128)(2,1)S(1)} %copy-done.1, f32[64,2048]{1,0:T(8,128)S(1)} %attn0.2.pa_ref, f32[64,2048]{1,0:T(8,128)S(1)} %collective-permute-done.pb_ref, bf16[2,2048]{1,0:T(2,128)(2,1)S(1)} %copy-done.4, bf16[2,2048]{1,0:T(2,128)(2,1)S(1)} %copy-done.3, ...), custom_call_target="tpu_custom_call" | custom-call | tf_op jit(solution)/shard_map/ffn0/pallas_call | solution.py:423
  95.9 17.4 %attn1.3 = f32[64,2048]{1,0:T(8,128)S(1)} custom-call(s32[1,128]{1,0:T(1,128)S(1)} %get-tuple-element.9.order_ref, s32[128]{0:T(128)S(1)} %copy-done.6, f32[5120,128]{1,0:T(8,128)S(1)} %get-tuple-element.12.q_ref, bf16[2,128,576,512]{3,2,1,0:T(8,128)(2,1)} %bitcast.1.ct_ref, bf16[2,4096,2048]{2,1,0:T(8,128)(2,1)} %wo_ref.7), custom_call_target="tpu_custom_call" | custom-call | flops 20000000000 | bytes 41943040 | tf_op jit(solution)/shard_map/attn1/pallas_call | solution.py:169
  113.4 2.5 %collective-permute-start.1 = (f32[64,2048]{1,0:T(8,128)S(1)}, f32[64,2048]{1,0:T(8,128)S(1)}, u32[]{:S(2)}, u32[]{:S(2)}) collective-permute-start(f32[64,2048]{1,0:T(8,128)S(1)} %attn1.3), channel_id=1, source_target_pairs={{0,4},{4,0},{1,5},{5,1},{2,6},{6,2},{3,7},{7,3}} | collective-permute-start | bytes 1572872 | tf_op jit(solution)/shard_map/ppermute | solution.py:445
  115.9 17.7 %attn1.2.pa_ref = f32[64,2048]{1,0:T(8,128)S(1)} custom-call(s32[1,128]{1,0:T(1,128)S(1)} %get-tuple-element.9.order_ref, s32[128]{0:T(128)S(1)} %copy-done.6, f32[5120,128]{1,0:T(8,128)S(1)} %get-tuple-element.12.q_ref, bf16[2,128,576,512]{3,2,1,0:T(8,128)(2,1)} %bitcast.1.ct_ref, bf16[2,4096,2048]{2,1,0:T(8,128)(2,1)} %wo_ref.7), custom_call_target="tpu_custom_call" | custom-call | flops 20000000000 | bytes 41943040 | tf_op jit(solution)/shard_map/attn1/pallas_call | solution.py:169
  133.6 0.0 collective-permute-done.1.pb_ref
  133.6 42.3 %ffn1.1 = bf16[128,2048]{1,0:T(8,128)(2,1)S(1)} custom-call(bf16[64,2048]{1,0:T(8,128)(2,1)S(1)} %get-tuple-element.11.xo_ref, f32[64,2048]{1,0:T(8,128)S(1)} %attn1.2.pa_ref, f32[64,2048]{1,0:T(8,128)S(1)} %collective-permute-done.1.pb_ref, bf16[2,2048]{1,0:T(2,128)(2,1)S(1)} %copy-done.4, bf16[2,2048]{1,0:T(2,128)(2,1)S(1)} %copy-done.3, ...), custom_call_target="tpu_custom_call" | custom-call | tf_op jit(solution)/shard_map/ffn1/pallas_call | solution.py:423
  175.9 0.8 copy.12
Async XLA Ops:
  0.0 1.0 copy-start
  1.0 0.7 copy-start.2
  1.7 0.7 copy-start.5
  2.4 7.6 %copy-start.6 = (s32[128]{0:T(128)S(1)}, s32[128]{0:T(128)}, u32[]{:S(2)}) copy-start(s32[128]{0:T(128)} %lens_ref.7) | copy-start | bytes 1540
  27.5 20.9 %copy-start.1 = (bf16[128,2048]{1,0:T(8,128)(2,1)S(1)}, bf16[128,2048]{1,0:T(8,128)(2,1)}, u32[]{:S(2)}) copy-start(bf16[128,2048]{1,0:T(8,128)(2,1)} %xo_ref.1) | copy-start | bytes 1572868
  27.5 20.9 %copy-start.3 = (bf16[2,2048]{1,0:T(2,128)(2,1)S(1)}, bf16[2,2048]{1,0:T(2,128)(2,1)}, u32[]{:S(2)}) copy-start(bf16[2,2048]{1,0:T(2,128)(2,1)} %an_ref.5) | copy-start | bytes 24580
  27.5 20.9 %copy-start.4 = (bf16[2,2048]{1,0:T(2,128)(2,1)S(1)}, bf16[2,2048]{1,0:T(2,128)(2,1)}, u32[]{:S(2)}) copy-start(bf16[2,2048]{1,0:T(2,128)(2,1)} %fn_ref.3) | copy-start | bytes 24580
  27.5 20.8 %collective-permute-start = (f32[64,2048]{1,0:T(8,128)S(1)}, f32[64,2048]{1,0:T(8,128)S(1)}, u32[]{:S(2)}, u32[]{:S(2)}) collective-permute-start(f32[64,2048]{1,0:T(8,128)S(1)} %attn0.3), channel_id=1, source_target_pairs={{0,4},{4,0},{1,5},{5,1},{2,6},{6,2},{3,7},{7,3}} | collective-permute-start | bytes 1572872 | tf_op jit(solution)/shard_map/ppermute | solution.py:445
  113.4 20.2 %collective-permute-start.1 = (f32[64,2048]{1,0:T(8,128)S(1)}, f32[64,2048]{1,0:T(8,128)S(1)}, u32[]{:S(2)}, u32[]{:S(2)}) collective-permute-start(f32[64,2048]{1,0:T(8,128)S(1)} %attn1.3), channel_id=1, source_target_pairs={{0,4},{4,0},{1,5},{5,1},{2,6},{6,2},{3,7},{7,3}} | collective-permute-start | bytes 1572872 | tf_op jit(solution)/shard_map/ppermute | solution.py:445

commit v4 on v3

--- a/solution.py
+++ b/solution.py
@@ -18,29 +18,38 @@
 ANY = pl.BlockSpec(memory_space=pl.ANY)
 
 
+PAD = 256
+
+
 def _rmsnorm(v, w):
     vf = v.astype(F32)
     r = lax.rsqrt(jnp.mean(vf * vf, axis=-1, keepdims=True) + EPS)
     return (vf * r * w.astype(F32)).astype(BF)
 
 
-def _project(h, w, j, q_ref, nb, nh, kv):
+def _project(h, w, j, q_ref, nb, kv):
     nblk = -(-kv // 128)
     val = jnp.dot(h, w, preferred_element_type=F32).astype(BF).astype(F32)
     lo = (kv // 128) * 128
     odd = pltpu.roll(val[:, lo:lo + nblk * 128], nblk * 128 - (kv - lo), 1)
     for t, v in ((0, val), (1, odd)):
         for i in range(nblk):
-            q_ref[pl.ds(i * nb * nh + 2 * j + t, nb, stride=nh), :] = v[:, i * 128:(i + 1) * 128]
-
-
-def _first_kernel(lens_ref, x_ref, an_ref, wq_ref, order_ref, q_ref, wbuf, wsem):
+            q_ref[pl.ds(((2 * j + t) * nblk + i) * nb, nb), :] = v[:, i * 128:(i + 1) * 128]
+
+
+def _first_kernel(lens_hbm, x_hbm, an_hbm, wq_ref, order_ref, q_ref, wbuf, wsem, lens_ref, x_ref, an_ref, isem):
     nb = x_ref.shape[0]
-    kv2 = wbuf.shape[2]
+    ins = [pltpu.make_async_copy(src, dst, isem.at[i])
+           for i, (src, dst) in enumerate(((lens_hbm, lens_ref), (x_hbm, x_ref), (an_hbm, an_ref)))]
+    for cp in ins:
+        cp.start()
+    kv2 = wq_ref.shape[2] // wbuf.shape[0]
     nj = wbuf.shape[0]
-    cps = [pltpu.make_async_copy(wq_ref.at[0, :, pl.ds(j * kv2, kv2)], wbuf.at[j], wsem.at[j]) for j in range(nj)]
+    cps = [pltpu.make_async_copy(wq_ref.at[0, :, pl.ds(j * kv2, kv2)], wbuf.at[j, :, pl.ds(0, kv2)], wsem.at[j]) for j in range(nj)]
     for cp in cps:
         cp.start()
+    for cp in ins:
+        cp.wait()
     tp = lax.axis_index("tp").astype(F32)
     half = nb // 2
     r = lax.broadcasted_iota(jnp.int32, (nb, nb), 0).astype(F32)
@@ -52,11 +61,13 @@
     rank = jnp.sum(jnp.where((rh == ch) & (key < mine), 1.0, 0.0), axis=1, keepdims=True)
     want = jnp.where(ch == 0.0, 1.0 - tp, tp)
     hit = (rank == c - ch * half) & (rh == want)
-    order_ref[...] = jnp.sum(jnp.where(hit, r, 0.0), axis=0, keepdims=True).astype(jnp.int32)
+    order_ref[0:1, :] = jnp.sum(jnp.where(hit, r, 0.0), axis=0, keepdims=True).astype(jnp.int32)
+    mylen = jnp.sum(jnp.where(r == c, jnp.broadcast_to(lens_ref[...].astype(F32), (nb, nb)), 0.0), axis=1, keepdims=True)
+    order_ref[1:2, :] = jnp.sum(jnp.where(hit, mylen, 0.0), axis=0, keepdims=True).astype(jnp.int32)
     h = _rmsnorm(x_ref[...], an_ref[0:1, :])
     for j in range(nj):
         cps[j].wait()
-        _project(h, wbuf[j], j, q_ref, nb, 2 * nj, kv2 // 2)
+        _project(h, wbuf[j, :, 0:kv2], j, q_ref, nb, kv2 // 2)
 
 
 def _first(lens, x, an, wq, nh):
@@ -64,18 +75,24 @@
     kv = wq.shape[2] // nh
     return pl.pallas_call(
         _first_kernel,
-        out_shape=[jax.ShapeDtypeStruct((1, nb), jnp.int32),
+        out_shape=[jax.ShapeDtypeStruct((2, nb), jnp.int32),
                    jax.ShapeDtypeStruct((-(-kv // 128) * nb * nh, 128), F32)],
-        in_specs=[VMEM, VMEM, VMEM, ANY],
+        in_specs=[ANY, ANY, ANY, ANY],
         out_specs=[VMEM, VMEM],
-        scratch_shapes=[pltpu.VMEM((nh // 2, d, 2 * kv), BF), pltpu.SemaphoreType.DMA((nh // 2,))],
+        scratch_shapes=[pltpu.VMEM((nh // 2, d, 2 * kv + 128), BF), pltpu.SemaphoreType.DMA((nh // 2,)),
+                        pltpu.VMEM((1, nb), jnp.int32), pltpu.VMEM((nb, d), BF), pltpu.VMEM(an.shape, BF),
+                        pltpu.SemaphoreType.DMA((3,))],
         compiler_params=pltpu.CompilerParams(vmem_limit_bytes=32 * 2 ** 20),
         name="first",
-    )(lens.reshape(1, nb), x, an, wq)
-
-
-def _attn_kernel(layer, off, nh, G, NS, order_ref, lens_ref, q_ref, ct_ref, wo_ref, out_ref,
-                 buf, sems, wbuf, wsems, o_s, oflat):
+    )(*[pltpu.with_memory_space_constraint(t, pltpu.HBM) for t in (lens.reshape(1, nb), x, an, wq)])
+
+
+def _attn_kernel(layer, off, nh, G, NS, order_ref, q_ref, ct_ref, wo_ref, out_ref, *rest):
+    if off == 0:
+        wbuf, buf, sems, o_s, oflat, wsems = rest
+    else:
+        buf, sems, o_s, oflat = rest
+        wbuf = wo_ref
     kv = ct_ref.shape[2]
     nmax = ct_ref.shape[3] // 128
     nb = out_ref.shape[0]
@@ -87,8 +104,11 @@
     def seq(i):
         return order_ref[0, off + i]
 
+    def length(i):
+        return order_ref[1, off + i]
+
     def chunks(g):
-        return lax.div(lens_ref[seq(g * G + G - 1)] + 127, 128)
+        return lax.div(length(g * G + G - 1) + 127, 128)
 
     def copies(g, n):
         slot = lax.rem(g, NS)
@@ -110,7 +130,7 @@
                     cp.start()
 
     def qrow(b):
-        parts = [q_ref[pl.ds(pl.multiple_of(i * nall * nh + b * nh, nh), nh), :] for i in range(qblk)]
+        parts = [q_ref[pl.ds(i * nall + b, nh, stride=qblk * nall), :] for i in range(qblk)]
         return jnp.concatenate(parts, axis=-1)[:, :kv].astype(BF)
 
     for g in range(NS - 1):
@@ -120,7 +140,8 @@
         @pl.when(g + NS - 1 < ng)
         def _():
             start(g + NS - 1)
-        wcopy(g).start()
+        if off == 0:
+            wcopy(g).start()
         c = chunks(g)
         slot = lax.rem(g, NS)
         for n in range(1, nmax + 1):
@@ -133,7 +154,7 @@
                 scs = [jnp.dot(qrow(bs[s]), buf[slot, s, :, 0:N], preferred_element_type=F32)
                        for s in range(G)]
                 pos = lax.broadcasted_iota(jnp.int32, (nh, N), 1)
-                scs = [jnp.where(pos < lens_ref[bs[s]], scs[s] * SCALE, -jnp.inf) for s in range(G)]
+                scs = [jnp.where(pos < length(g * G + s), scs[s] * SCALE, -jnp.inf) for s in range(G)]
                 ms = [jnp.max(sc, axis=-1, keepdims=True) for sc in scs]
                 es = [jnp.exp(sc - m) for sc, m in zip(scs, ms)]
                 ds = [jnp.sum(e, axis=-1, keepdims=True) for e in es]
@@ -141,17 +162,17 @@
                 outs = [lax.dot_general(ps[s], buf[slot, s, 0:LAT, 0:N], (((1,), (1,)), ((), ())),
                                         preferred_element_type=F32) for s in range(G)]
                 for s in range(G):
-                    row = lax.rem(bs[s], nb) * nh
+                    row = lax.rem(bs[s], nb)
                     for i in range(LAT // 128):
-                        o_s[pl.ds(pl.multiple_of(row + i * nb * nh, nh), nh), :] = outs[s][:, i * 128:(i + 1) * 128]
+                        o_s[pl.ds(row + i * nb, nh, stride=LAT // 128 * nb), :] = outs[s][:, i * 128:(i + 1) * 128]
         return carry
 
     lax.fori_loop(0, ng, body, 0)
     for h in range(nh):
         for i in range(LAT // 128):
             c = h * LAT + i * 128
-            oflat[:, c:c + 128] = o_s[pl.ds(i * nb * nh + h, nb, stride=nh), :].astype(BF)
-    for g in range(ng):
+            oflat[:, c:c + 128] = o_s[pl.ds((h * (LAT // 128) + i) * nb, nb), :].astype(BF)
+    for g in range(ng if off == 0 else 0):
         wcopy(g).wait()
     nblk = 1024
 
@@ -162,24 +183,24 @@
     lax.fori_loop(0, out_ref.shape[1] // nblk, mm, 0)
 
 
-def _attention(layer, off, q, ct, order, lens, wo, nh, G=8, NS=3):
+def _attention(layer, off, q, ct, order, wo, nh, G=8, NS=3):
     kv, s_len = ct.shape[2:]
     nb = order.shape[1] // 2
-    hid, d = wo.shape[1], wo.shape[2]
+    hid, d = wo.shape[-2:]
+    part = jax.ShapeDtypeStruct((nb, d), F32)
     return pl.pallas_call(
         functools.partial(_attn_kernel, layer, off, nh, G, NS),
-        out_shape=jax.ShapeDtypeStruct((nb, d), F32),
-        in_specs=[SMEM, SMEM, VMEM, ANY, ANY],
-        out_specs=VMEM,
+        out_shape=[part, jax.ShapeDtypeStruct((hid, d), BF)] if off == 0 else part,
+        in_specs=[SMEM, VMEM, ANY, ANY if off == 0 else VMEM],
+        out_specs=[VMEM, VMEM] if off == 0 else VMEM,
         scratch_shapes=[
             pltpu.VMEM((NS, G, kv, s_len), BF), pltpu.SemaphoreType.DMA((NS, G)),
-            pltpu.VMEM((hid, d), BF), pltpu.SemaphoreType.DMA((nb // G,)),
             pltpu.VMEM((LAT // 128 * nb * nh, 128), F32), pltpu.VMEM((nb, hid), BF),
-        ],
-        compiler_params=pltpu.CompilerParams(vmem_limit_bytes=40 * 2 ** 20),
+        ] + ([pltpu.SemaphoreType.DMA((nb // G,))] if off == 0 else []),
+        compiler_params=pltpu.CompilerParams(vmem_limit_bytes=24 * 2 ** 20),
         cost_estimate=pl.CostEstimate(flops=20 * 10 ** 9, bytes_accessed=40 * 2 ** 20, transcendentals=0),
         name=f"attn{layer}",
-    )(order, lens, q, ct, wo)
+    )(order, q, ct, wo)
 
 
 XLOC = {1: (1, 0), 0: (2, 0)}
@@ -217,14 +238,15 @@
             wcopies.append(pltpu.make_async_copy(
                 w.at[layer, :, pl.ds(j * 128, 128)], w13.at[:, pl.ds(j * 256 + i * 128, 128)],
                 wsem.at[j, i]))
-    w2copy = pltpu.make_async_copy(w2_ref.at[layer], w2v, w2sem)
+    w2copy = pltpu.make_async_copy(w2_ref.at[layer], w2v.at[:, pl.ds(0, w2_ref.shape[2])], w2sem)
     for cp in wcopies:
         cp.start()
     w2copy.start()
     nj = nh // 2
     if not last:
         kv2 = wq_ref.shape[2] // nj
-        dst = [w13.at[:, pl.ds(j * kv2, kv2)] if j < 2 else wqv.at[j - 2] for j in range(nj)]
+        dst = [w13.at[:, pl.ds(j * kv2, kv2)] if j < 2 else wqv.at[j - 2, :, pl.ds(0, kv2)]
+               for j in range(nj)]
         wqcopies = [pltpu.make_async_copy(wq_ref.at[layer + 1, :, pl.ds(j * kv2, kv2)], dst[j], wqsem.at[j])
                     for j in range(nj)]
         for cp in wqcopies[2:]:
@@ -386,7 +408,7 @@
         h = _rmsnorm(xall[...], an_ref[layer + 1:layer + 2, :])
         for j, cp in enumerate(wqcopies):
             cp.wait()
-            _project(h, dst[j][...], j, q_ref, 2 * HALF, nh, kv2 // 2)
+            _project(h, dst[j][...], j, q_ref, 2 * HALF, kv2 // 2)
     for cp in [own_sib, relay_x, relay_y, *own_x.values(), *own_y.values(), *sib_g.values(),
                *st1_x.values(), *st1_y.values(), *st1_dx.values(), *st1_dy.values(),
                *st2_x.values(), *st2_y.values(), *xg.values()]:
@@ -410,8 +432,8 @@
                      jax.ShapeDtypeStruct((-(-kv // 128) * 2 * rows * nh, 128), F32)]
     NA, NB = len(A), len(B)
     scratch = [
-        pltpu.VMEM((d, 2 * f), BF), pltpu.VMEM((f, d), BF),
-        pltpu.VMEM((1, 16, 128) if last else (nh // 2 - 2, d, 2 * kv), BF),
+        pltpu.VMEM((d, 2 * f), BF), pltpu.VMEM((f, d + PAD), BF),
+        pltpu.VMEM((1, 16, 128) if last else (nh // 2 - 2, d, 2 * kv + 128), BF),
         pltpu.VMEM((4, 2, 2, 32, d), BF), pltpu.VMEM((4, 2, 2, 32, d), F32), pltpu.VMEM((4, 2, 32, d), F32),
         pltpu.VMEM((128, f), BF), pltpu.VMEM((rows, d), BF), pltpu.VMEM((2 * rows, d), BF),
         pltpu.VMEM((2, 32, NA * W), F32), pltpu.VMEM((2, NA, 32, W), F32),
@@ -427,7 +449,7 @@
         out_specs=[VMEM] * len(out_shape),
         scratch_shapes=scratch,
         compiler_params=pltpu.CompilerParams(collective_id=layer, has_side_effects=True,
-                                             vmem_limit_bytes=46 * 2 ** 20),
+                                             vmem_limit_bytes=48 * 2 ** 20),
         name=f"ffn{layer}",
     )(xo, pa, pb, fn, an, w1, w3, w2, wq)
 
@@ -441,9 +463,9 @@
         order, q = _first(lengths, x, attn_norm, wq, nh)
         for l in range(n_layers):
             last = l == n_layers - 1
-            pa = _attention(l, 0, q, ct, order, lengths, wo, nh)
+            pa, wo_l = _attention(l, 0, q, ct, order, wo, nh)
             pa = lax.ppermute(pa, 'tp', [(0, 1), (1, 0)])
-            pb = _attention(l, nb // 2, q, ct, order, lengths, wo, nh)
+            pb = _attention(l, nb // 2, q, ct, order, wo_l, nh)
             res = _ffn(l, last, nh, x, pb, pa, ffn_norm, attn_norm, w1, w3, w2, wq)
             if last:
                 return res[0]

time: 176 us -> 175 us (level)
  starting transfers between devices: 5.91 us -> 10.2 us
  Pallas kernels: 167 us -> 163 us
  local copies, waits for them, and re-layouts: 3.21 us -> 0.81 us
    pallas_call x2, Pallas kernels: 89.9 us -> 83.1 us  [_ffn(): pl.pallas_call(functools.partial(_ffn_kernel, layer, last, nh), out_shape...]
    ppermute x2, starting transfers between devices: 5.91 us -> 10.2 us  [body(): pa = lax.ppermute(pa, 'tp', [(0, 1), (1, 0)])]
    unnamed x15 -> x7, local copies, waits for them, and re-layouts: 3.21 us -> 0.81 us
  transfers between devices with their start and end apart: 2 -> 2, of which waited for: 0 -> 0; matrix products, arithmetic and copies ran while one was open for 0% -> 0% of each run, Pallas kernels for 20% -> 21%
where the time goes in v4:
time: 175 us; the launch traced here: 174 us
  Pallas kernels  163 us (93%)
  starting transfers between devices  10.2 us (6%)
    pallas_call x2, Pallas kernels, _ffn(): pl.pallas_call(functools.partial(_ffn_kernel, layer, last, nh), out_shape...  83.1 us
    pallas_call x4, Pallas kernels, _attention(): pl.pallas_call(functools.partial(_attn_kernel, layer, off, nh, G, NS), ou...  70.9 us
    ppermute x2, starting transfers between devices, body(): pa = lax.ppermute(pa, 'tp', [(0, 1), (1, 0)])  10.2 us
    pallas_call x1, Pallas kernels, _first(): pl.pallas_call(_first_kernel, out_shape=[jax.ShapeDtypeStruct((2, nb), jn...  9.07 us
  transfers between devices with their start and end apart: 2, of which 0 were waited for; matrix products, arithmetic and copies ran while one was open for 0% of the time, Pallas kernels for 21%

profile of v4, /device:TPU:0, one launch (start us, length us, event | category | flops | bytes accessed | tf_op | source)
XLA Modules:
  0.0 174.2 jit_solution(10732794858981470463)
XLA Ops:
  0.0 9.1 %first.1 = (s32[2,128]{1,0:T(2,128)S(1)}, f32[5120,128]{1,0:T(8,128)S(1)}) custom-call(s32[1,128]{1,0:T(1,128)} %bitcast.2, bf16[128,2048]{1,0:T(8,128)(2,1)} %xo_ref.1, bf16[2,2048]{1,0:T(2,128)(2,1)} %an_ref.3, bf16[2,2048,4608]{2,1,0:T(8,128)(2,1)} %wq_ref.5), custom_call_target="tpu_custom_call" | custom-call | tf_op jit(solution)/shard_map/first/pallas_call | solution.py:76
  9.1 16.7 %attn0.2 = (f32[64,2048]{1,0:T(8,128)S(1)}, bf16[4096,2048]{1,0:T(8,128)(2,1)S(1)}) custom-call(s32[2,128]{1,0:T(2,128)S(1)} %get-tuple-element.13.order_ref, f32[5120,128]{1,0:T(8,128)S(1)} %get-tuple-element.14.q_ref, bf16[2,128,576,512]{3,2,1,0:T(8,128)(2,1)} %bitcast.1.ct_ref, bf16[2,4096,2048]{2,1,0:T(8,128)(2,1)} %wo_ref.3), custom_call_target="tpu_custom_call" | custom-call | flops 20000000000 | bytes 41943040 | tf_op jit(solution)/shard_map/attn0/pallas_call | solution.py:191
  25.8 5.4 %collective-permute-start = (f32[64,2048]{1,0:T(8,128)S(1)}, f32[64,2048]{1,0:T(8,128)S(1)}, u32[]{:S(2)}, u32[]{:S(2)}) collective-permute-start(f32[64,2048]{1,0:T(8,128)S(1)} %get-tuple-element.16), channel_id=1, source_target_pairs={{0,4},{4,0},{1,5},{5,1},{2,6},{6,2},{3,7},{7,3}} | collective-permute-start | bytes 1572872 | tf_op jit(solution)/shard_map/ppermute | solution.py:467
  31.3 0.0 copy-start
  31.3 0.0 copy-start.1
  31.3 0.0 copy-start.2
  31.3 18.6 %attn0.3.pa_ref = f32[64,2048]{1,0:T(8,128)S(1)} custom-call(s32[2,128]{1,0:T(2,128)S(1)} %get-tuple-element.13.order_ref, f32[5120,128]{1,0:T(8,128)S(1)} %get-tuple-element.14.q_ref, bf16[2,128,576,512]{3,2,1,0:T(8,128)(2,1)} %bitcast.1.ct_ref, bf16[4096,2048]{1,0:T(8,128)(2,1)S(1)} %get-tuple-element.15.wo_ref), custom_call_target="tpu_custom_call" | custom-call | flops 20000000000 | bytes 41943040 | tf_op jit(solution)/shard_map/attn0/pallas_call | solution.py:191
  49.8 0.0 collective-permute-done.pb_ref
  49.8 0.0 copy-done
  49.8 0.0 copy-done.1
  49.9 0.0 copy-done.2
  49.9 43.8 %ffn0.1 = (bf16[64,2048]{1,0:T(8,128)(2,1)S(1)}, f32[5120,128]{1,0:T(8,128)S(1)}) custom-call(bf16[128,2048]{1,0:T(8,128)(2,1)S(1)} %copy-done, f32[64,2048]{1,0:T(8,128)S(1)} %attn0.3.pa_ref, f32[64,2048]{1,0:T(8,128)S(1)} %collective-permute-done.pb_ref, bf16[2,2048]{1,0:T(2,128)(2,1)S(1)} %copy-done.2, bf16[2,2048]{1,0:T(2,128)(2,1)S(1)} %copy-done.1, ...), custom_call_target="tpu_custom_call" | custom-call | tf_op jit(solution)/shard_map/ffn0/pallas_call | solution.py:445
  93.7 17.0 %attn1.2 = (f32[64,2048]{1,0:T(8,128)S(1)}, bf16[4096,2048]{1,0:T(8,128)(2,1)S(1)}) custom-call(s32[2,128]{1,0:T(2,128)S(1)} %get-tuple-element.13.order_ref, f32[5120,128]{1,0:T(8,128)S(1)} %get-tuple-element.18.q_ref, bf16[2,128,576,512]{3,2,1,0:T(8,128)(2,1)} %bitcast.1.ct_ref, bf16[2,4096,2048]{2,1,0:T(8,128)(2,1)} %wo_ref.3), custom_call_target="tpu_custom_call" | custom-call | flops 20000000000 | bytes 41943040 | tf_op jit(solution)/shard_map/attn1/pallas_call | solution.py:191
  110.7 4.8 %collective-permute-start.1 = (f32[64,2048]{1,0:T(8,128)S(1)}, f32[64,2048]{1,0:T(8,128)S(1)}, u32[]{:S(2)}, u32[]{:S(2)}) collective-permute-start(f32[64,2048]{1,0:T(8,128)S(1)} %get-tuple-element.20), channel_id=1, source_target_pairs={{0,4},{4,0},{1,5},{5,1},{2,6},{6,2},{3,7},{7,3}} | collective-permute-start | bytes 1572872 | tf_op jit(solution)/shard_map/ppermute | solution.py:467
  115.4 18.6 %attn1.3.pa_ref = f32[64,2048]{1,0:T(8,128)S(1)} custom-call(s32[2,128]{1,0:T(2,128)S(1)} %get-tuple-element.13.order_ref, f32[5120,128]{1,0:T(8,128)S(1)} %get-tuple-element.18.q_ref, bf16[2,128,576,512]{3,2,1,0:T(8,128)(2,1)} %bitcast.1.ct_ref, bf16[4096,2048]{1,0:T(8,128)(2,1)S(1)} %get-tuple-element.19.wo_ref), custom_call_target="tpu_custom_call" | custom-call | flops 20000000000 | bytes 41943040 | tf_op jit(solution)/shard_map/attn1/pallas_call | solution.py:191
  134.0 0.0 collective-permute-done.1.pb_ref
  134.0 39.3 %ffn1.1 = bf16[128,2048]{1,0:T(8,128)(2,1)S(1)} custom-call(bf16[64,2048]{1,0:T(8,128)(2,1)S(1)} %get-tuple-element.17.xo_ref, f32[64,2048]{1,0:T(8,128)S(1)} %attn1.3.pa_ref, f32[64,2048]{1,0:T(8,128)S(1)} %collective-permute-done.1.pb_ref, bf16[2,2048]{1,0:T(2,128)(2,1)S(1)} %copy-done.2, bf16[2,2048]{1,0:T(2,128)(2,1)S(1)} %copy-done.1, ...), custom_call_target="tpu_custom_call" | custom-call | tf_op jit(solution)/shard_map/ffn1/pallas_call | solution.py:445
  173.4 0.8 copy.12
Async XLA Ops:
  25.8 24.0 %collective-permute-start = (f32[64,2048]{1,0:T(8,128)S(1)}, f32[64,2048]{1,0:T(8,128)S(1)}, u32[]{:S(2)}, u32[]{:S(2)}) collective-permute-start(f32[64,2048]{1,0:T(8,128)S(1)} %get-tuple-element.16), channel_id=1, source_target_pairs={{0,4},{4,0},{1,5},{5,1},{2,6},{6,2},{3,7},{7,3}} | collective-permute-start | bytes 1572872 | tf_op jit(solution)/shard_map/ppermute | solution.py:467
  31.3 18.6 %copy-start = (bf16[128,2048]{1,0:T(8,128)(2,1)S(1)}, bf16[128,2048]{1,0:T(8,128)(2,1)}, u32[]{:S(2)}) copy-start(bf16[128,2048]{1,0:T(8,128)(2,1)} %xo_ref.1) | copy-start | bytes 1572868
  31.3 18.6 %copy-start.1 = (bf16[2,2048]{1,0:T(2,128)(2,1)S(1)}, bf16[2,2048]{1,0:T(2,128)(2,1)}, u32[]{:S(2)}) copy-start(bf16[2,2048]{1,0:T(2,128)(2,1)} %an_ref.3) | copy-start | bytes 24580
  31.3 18.6 %copy-start.2 = (bf16[2,2048]{1,0:T(2,128)(2,1)S(1)}, bf16[2,2048]{1,0:T(2,128)(2,1)}, u32[]{:S(2)}) copy-start(bf16[2,2048]{1,0:T(2,128)(2,1)} %fn_ref.3) | copy-start | bytes 24580
  110.7 23.3 %collective-permute-start.1 = (f32[64,2048]{1,0:T(8,128)S(1)}, f32[64,2048]{1,0:T(8,128)S(1)}, u32[]{:S(2)}, u32[]{:S(2)}) collective-permute-start(f32[64,2048]{1,0:T(8,128)S(1)} %get-tuple-element.20), channel_id=1, source_target_pairs={{0,4},{4,0},{1,5},{5,1},{2,6},{6,2},{3,7},{7,3}} | collective-permute-start | bytes 1572872 | tf_op jit(solution)/shard_map/ppermute | solution.py:467

commit v5 on v4

--- a/solution.py
+++ b/solution.py
@@ -16,9 +16,6 @@
 VMEM = pl.BlockSpec(memory_space=pltpu.VMEM)
 SMEM = pl.BlockSpec(memory_space=pltpu.SMEM)
 ANY = pl.BlockSpec(memory_space=pl.ANY)
-
-
-PAD = 256
 
 
 def _rmsnorm(v, w):
@@ -84,14 +81,14 @@
                         pltpu.SemaphoreType.DMA((3,))],
         compiler_params=pltpu.CompilerParams(vmem_limit_bytes=32 * 2 ** 20),
         name="first",
-    )(*[pltpu.with_memory_space_constraint(t, pltpu.HBM) for t in (lens.reshape(1, nb), x, an, wq)])
-
-
-def _attn_kernel(layer, off, nh, G, NS, order_ref, q_ref, ct_ref, wo_ref, out_ref, *rest):
-    if off == 0:
-        wbuf, buf, sems, o_s, oflat, wsems = rest
+    )(*[pltpu.with_memory_space_constraint(t, pltpu.HBM) for t in (lens.reshape(1, nb), x, an)], wq)
+
+
+def _attn_kernel(layer, off, load, nh, G, NS, order_ref, q_ref, ct_ref, wo_ref, *rest):
+    if load:
+        out_ref, buf, wbuf, sems, o_s, oflat, wsems = rest
     else:
-        buf, sems, o_s, oflat = rest
+        out_ref, buf, sems, o_s, oflat = rest if off == 0 else rest[1:]
         wbuf = wo_ref
     kv = ct_ref.shape[2]
     nmax = ct_ref.shape[3] // 128
@@ -101,11 +98,14 @@
     wrows = wbuf.shape[0] // ng
     qblk = -(-kv // 128)
 
+    base = off // G
+    ahead = NS - 1
+
     def seq(i):
-        return order_ref[0, off + i]
+        return order_ref[0, i]
 
     def length(i):
-        return order_ref[1, off + i]
+        return order_ref[1, i]
 
     def chunks(g):
         return lax.div(length(g * G + G - 1) + 127, 128)
@@ -133,23 +133,32 @@
         parts = [q_ref[pl.ds(i * nall + b, nh, stride=qblk * nall), :] for i in range(qblk)]
         return jnp.concatenate(parts, axis=-1)[:, :kv].astype(BF)
 
-    for g in range(NS - 1):
-        start(g)
+    if off == 0:
+        for g in range(ahead):
+            start(g)
 
     def body(g, carry):
-        @pl.when(g + NS - 1 < ng)
-        def _():
-            start(g + NS - 1)
         if off == 0:
-            wcopy(g).start()
+            start(g + ahead)
+            if load:
+                wcopy(g).start()
+        else:
+            @pl.when(g + ahead < base + ng)
+            def _():
+                start(g + ahead)
         c = chunks(g)
         slot = lax.rem(g, NS)
         for n in range(1, nmax + 1):
             @pl.when(c == n)
             def _():
                 N = n * 128
-                for cp in copies(g, n):
-                    cp.wait()
+                def arrived():
+                    for cp in copies(g, n):
+                        cp.wait()
+                if off == 0:
+                    arrived()
+                else:
+                    pl.when(g >= base + ahead)(arrived)
                 bs = [seq(g * G + s) for s in range(G)]
                 scs = [jnp.dot(qrow(bs[s]), buf[slot, s, :, 0:N], preferred_element_type=F32)
                        for s in range(G)]
@@ -167,13 +176,21 @@
                         o_s[pl.ds(row + i * nb, nh, stride=LAT // 128 * nb), :] = outs[s][:, i * 128:(i + 1) * 128]
         return carry
 
-    lax.fori_loop(0, ng, body, 0)
+    lax.fori_loop(base, base + ng, body, 0)
     for h in range(nh):
         for i in range(LAT // 128):
             c = h * LAT + i * 128
             oflat[:, c:c + 128] = o_s[pl.ds((h * (LAT // 128) + i) * nb, nb), :].astype(BF)
-    for g in range(ng if off == 0 else 0):
-        wcopy(g).wait()
+    if off == 0:
+        for g in range(ng if load else 0):
+            wcopy(g).wait()
+        for g in range(ng, ng + ahead):
+            c = chunks(g)
+            for n in range(1, nmax + 1):
+                @pl.when(c == n)
+                def _():
+                    for cp in copies(g, n):
+                        cp.wait()
     nblk = 1024
 
     def mm(j, carry):
@@ -183,24 +200,28 @@
     lax.fori_loop(0, out_ref.shape[1] // nblk, mm, 0)
 
 
-def _attention(layer, off, q, ct, order, wo, nh, G=8, NS=3):
+def _attention(layer, off, q, ct, order, wo, nh, ring=None, G=8, NS=3):
     kv, s_len = ct.shape[2:]
     nb = order.shape[1] // 2
     hid, d = wo.shape[-2:]
+    first = off == 0
+    load = wo.ndim == 3
     part = jax.ShapeDtypeStruct((nb, d), F32)
+    rings = jax.ShapeDtypeStruct((NS, G, kv, s_len), BF)
     return pl.pallas_call(
-        functools.partial(_attn_kernel, layer, off, nh, G, NS),
-        out_shape=[part, jax.ShapeDtypeStruct((hid, d), BF)] if off == 0 else part,
-        in_specs=[SMEM, VMEM, ANY, ANY if off == 0 else VMEM],
-        out_specs=[VMEM, VMEM] if off == 0 else VMEM,
+        functools.partial(_attn_kernel, layer, off, load, nh, G, NS),
+        out_shape=[part, rings] + ([jax.ShapeDtypeStruct((hid, d), BF)] if load else []),
+        in_specs=[SMEM, VMEM, ANY, ANY if load else VMEM] + ([] if first else [VMEM]),
+        out_specs=[VMEM] * (3 if load else 2),
+        input_output_aliases={} if first else {4: 1},
         scratch_shapes=[
-            pltpu.VMEM((NS, G, kv, s_len), BF), pltpu.SemaphoreType.DMA((NS, G)),
+            pltpu.SemaphoreType.DMA((NS, G)),
             pltpu.VMEM((LAT // 128 * nb * nh, 128), F32), pltpu.VMEM((nb, hid), BF),
-        ] + ([pltpu.SemaphoreType.DMA((nb // G,))] if off == 0 else []),
-        compiler_params=pltpu.CompilerParams(vmem_limit_bytes=24 * 2 ** 20),
+        ] + ([pltpu.SemaphoreType.DMA((nb // G,))] if load else []),
+        compiler_params=pltpu.CompilerParams(vmem_limit_bytes=8 * 2 ** 20),
         cost_estimate=pl.CostEstimate(flops=20 * 10 ** 9, bytes_accessed=40 * 2 ** 20, transcendentals=0),
         name=f"attn{layer}",
-    )(order, q, ct, wo)
+    )(order, q, ct, wo, *([] if first else [ring]))
 
 
 XLOC = {1: (1, 0), 0: (2, 0)}
@@ -212,14 +233,14 @@
 HALF = 64
 
 
-def _ffn_kernel(layer, last, nh, xo_ref, pa_ref, pb_ref, fn_ref, an_ref, w1_ref, w3_ref, w2_ref, wq_ref, *rest):
+def _ffn_kernel(layer, last, nh, xo_ref, pa_ref, pb_ref, fn_ref, an_ref, w1_ref, w3_ref, w2_ref, wq_ref, wo_ref, *rest):
     if last:
         out_ref, rest = rest[0], rest[1:]
     else:
-        xn_ref, q_ref, rest = rest[0], rest[1], rest[2:]
-    (w13, w2v, wqv, gbuf, ybuf, sbuf, abuf, xp, xall,
+        xn_ref, q_ref, won_ref, rest = rest[0], rest[1], rest[2], rest[3:]
+    (w13, w2b, gbuf, ybuf, sbuf, abuf, xp, xall,
      r1x_own, r1x_y, r1y_own, r1y_x, r2x, r2y,
-     wsem, w2sem, wqsem, ss, rs) = rest
+     wsem, w2sem, wqsem, wosem, ss, rs) = rest
     tp = lax.axis_index("tp")
     dp = lax.axis_index("dp")
     xi, ci = lax.div(dp, 2), lax.rem(dp, 2)
@@ -238,19 +259,17 @@
             wcopies.append(pltpu.make_async_copy(
                 w.at[layer, :, pl.ds(j * 128, 128)], w13.at[:, pl.ds(j * 256 + i * 128, 128)],
                 wsem.at[j, i]))
-    w2copy = pltpu.make_async_copy(w2_ref.at[layer], w2v.at[:, pl.ds(0, w2_ref.shape[2])], w2sem)
+    w2copy = pltpu.make_async_copy(w2_ref.at[layer], w2b.at[pl.ds(0, w2_ref.shape[1]), pl.ds(0, w2_ref.shape[2])], w2sem)
     for cp in wcopies:
         cp.start()
     w2copy.start()
     nj = nh // 2
     if not last:
         kv2 = wq_ref.shape[2] // nj
-        dst = [w13.at[:, pl.ds(j * kv2, kv2)] if j < 2 else wqv.at[j - 2, :, pl.ds(0, kv2)]
-               for j in range(nj)]
+        dst = [(w13 if j < 2 else w2b).at[:, pl.ds(j % 2 * kv2, kv2)] for j in range(nj)]
         wqcopies = [pltpu.make_async_copy(wq_ref.at[layer + 1, :, pl.ds(j * kv2, kv2)], dst[j], wqsem.at[j])
                     for j in range(nj)]
-        for cp in wqcopies[2:]:
-            cp.start()
+        wocopy = pltpu.make_async_copy(wo_ref.at[layer + 1], won_ref, wosem)
 
     count = [16]
 
@@ -358,12 +377,16 @@
 
         a = abuf[...]
         for q in QORDER:
-            y = jnp.dot(a, w2v[:, q * W:(q + 1) * W], preferred_element_type=F32)
+            y = jnp.dot(a, w2b[0:w2_ref.shape[1], q * W:(q + 1) * W], preferred_element_type=F32)
             ybuf[k, :, :, :, q * W:(q + 1) * W] = y.reshape(2, 2, 32, W)
             sib_y(k, q).start()
         return carry
 
     lax.fori_loop(0, 4, chunk, 0)
+    if not last:
+        for cp in wqcopies[2:]:
+            cp.start()
+        wocopy.start()
     for q in QORDER:
         combine(3, q)
         for p in PS:
@@ -409,6 +432,8 @@
         for j, cp in enumerate(wqcopies):
             cp.wait()
             _project(h, dst[j][...], j, q_ref, 2 * HALF, kv2 // 2)
+    if not last:
+        wocopy.wait()
     for cp in [own_sib, relay_x, relay_y, *own_x.values(), *own_y.values(), *sib_g.values(),
                *st1_x.values(), *st1_y.values(), *st1_dx.values(), *st1_dy.values(),
                *st2_x.values(), *st2_y.values(), *xg.values()]:
@@ -421,7 +446,7 @@
 NCOPY = 16 + 10 + 4 + 8 + 8 + 8
 
 
-def _ffn(layer, last, nh, xo, pa, pb, fn, an, w1, w3, w2, wq):
+def _ffn(layer, last, nh, xo, pa, pb, fn, an, w1, w3, w2, wq, wo):
     rows, d = pa.shape
     f = w1.shape[2]
     kv = wq.shape[2] // nh
@@ -429,29 +454,29 @@
         out_shape = [jax.ShapeDtypeStruct((2 * rows, d), BF)]
     else:
         out_shape = [jax.ShapeDtypeStruct((rows, d), BF),
-                     jax.ShapeDtypeStruct((-(-kv // 128) * 2 * rows * nh, 128), F32)]
+                     jax.ShapeDtypeStruct((-(-kv // 128) * 2 * rows * nh, 128), F32),
+                     jax.ShapeDtypeStruct(wo.shape[1:], BF)]
     NA, NB = len(A), len(B)
     scratch = [
-        pltpu.VMEM((d, 2 * f), BF), pltpu.VMEM((f, d + PAD), BF),
-        pltpu.VMEM((1, 16, 128) if last else (nh // 2 - 2, d, 2 * kv + 128), BF),
+        pltpu.VMEM((d, 2 * f), BF), pltpu.VMEM((f, d) if last else (d, 4 * kv), BF),
         pltpu.VMEM((4, 2, 2, 32, d), BF), pltpu.VMEM((4, 2, 2, 32, d), F32), pltpu.VMEM((4, 2, 32, d), F32),
         pltpu.VMEM((128, f), BF), pltpu.VMEM((rows, d), BF), pltpu.VMEM((2 * rows, d), BF),
         pltpu.VMEM((2, 32, NA * W), F32), pltpu.VMEM((2, NA, 32, W), F32),
         pltpu.VMEM((2, 32, NB * W), F32), pltpu.VMEM((2, NB, 32, W), F32),
         pltpu.VMEM((2, NB, 32, W), F32), pltpu.VMEM((2, NA, 32, W), F32),
         pltpu.SemaphoreType.DMA((f // 128, 2)), pltpu.SemaphoreType.DMA, pltpu.SemaphoreType.DMA((nh // 2,)),
-        pltpu.SemaphoreType.DMA((NCOPY,)), pltpu.SemaphoreType.DMA((NCOPY,)),
+        pltpu.SemaphoreType.DMA, pltpu.SemaphoreType.DMA((NCOPY,)), pltpu.SemaphoreType.DMA((NCOPY,)),
     ]
     return pl.pallas_call(
         functools.partial(_ffn_kernel, layer, last, nh),
         out_shape=out_shape,
-        in_specs=[VMEM, VMEM, VMEM, VMEM, VMEM, ANY, ANY, ANY, ANY],
+        in_specs=[VMEM, VMEM, VMEM, VMEM, VMEM, ANY, ANY, ANY, ANY, ANY],
         out_specs=[VMEM] * len(out_shape),
         scratch_shapes=scratch,
         compiler_params=pltpu.CompilerParams(collective_id=layer, has_side_effects=True,
-                                             vmem_limit_bytes=48 * 2 ** 20),
+                                             vmem_limit_bytes=65 * 2 ** 19),
         name=f"ffn{layer}",
-    )(xo, pa, pb, fn, an, w1, w3, w2, wq)
+    )(xo, pa, pb, fn, an, w1, w3, w2, wq, wo)
 
 
 def solution(mesh):
@@ -460,16 +485,20 @@
         n_layers, _, s_len, kv = cache.shape
         nh = wq.shape[2] // kv
         ct = jnp.swapaxes(cache, 2, 3)
+        ct, wq, wo, w1, w3, w2 = [pltpu.with_memory_space_constraint(t, pltpu.HBM) for t in (ct, wq, wo, w1, w3, w2)]
         order, q = _first(lengths, x, attn_norm, wq, nh)
         for l in range(n_layers):
             last = l == n_layers - 1
-            pa, wo_l = _attention(l, 0, q, ct, order, wo, nh)
+            if l == 0:
+                pa, ring, wo_l = _attention(l, 0, q, ct, order, wo, nh)
+            else:
+                pa, ring = _attention(l, 0, q, ct, order, wo_l, nh)
             pa = lax.ppermute(pa, 'tp', [(0, 1), (1, 0)])
-            pb = _attention(l, nb // 2, q, ct, order, wo_l, nh)
-            res = _ffn(l, last, nh, x, pb, pa, ffn_norm, attn_norm, w1, w3, w2, wq)
+            pb, _ = _attention(l, nb // 2, q, ct, order, wo_l, nh, ring)
+            res = _ffn(l, last, nh, x, pb, pa, ffn_norm, attn_norm, w1, w3, w2, wq, wo)
             if last:
                 return res[0]
-            x, q = res
+            x, q, wo_l = res
 
     in_specs = (
         P('dp', None),

time: 175 us -> 172 us (0.983)
  starting transfers between devices: 10.2 us -> 4.21 us
  Pallas kernels: 163 us -> 167 us
    ppermute x2, starting transfers between devices: 10.2 us -> 4.21 us  [body(): pa = lax.ppermute(pa, 'tp', [(0, 1), (1, 0)])]
    pallas_call x2, Pallas kernels: 83.1 us -> 88.6 us  [_ffn(): pl.pallas_call(functools.partial(_ffn_kernel, layer, last, nh), out_shape...]
  transfers between devices with their start and end apart: 2 -> 2, of which waited for: 0 -> 0; matrix products, arithmetic and copies ran while one was open for 0% -> 0% of each run, Pallas kernels for 21% -> 19%
where the time goes in v5:
time: 172 us
  Pallas kernels  167 us (97%)
  starting transfers between devices  4.21 us (2%)
    pallas_call x2, Pallas kernels, _ffn(): pl.pallas_call(functools.partial(_ffn_kernel, layer, last, nh), out_shape...  88.6 us
    pallas_call x4, Pallas kernels, _attention(): pl.pallas_call(functools.partial(_attn_kernel, layer, off, load, nh, G, N...  69.5 us
    pallas_call x1, Pallas kernels, _first(): pl.pallas_call(_first_kernel, out_shape=[jax.ShapeDtypeStruct((2, nb), jn...  9.07 us
    ppermute x2, starting transfers between devices, body(): pa = lax.ppermute(pa, 'tp', [(0, 1), (1, 0)])  4.21 us
  transfers between devices with their start and end apart: 2, of which 0 were waited for; matrix products, arithmetic and copies ran while one was open for 0% of the time, Pallas kernels for 19%

profile of v5, /device:TPU:0, one launch (start us, length us, event | category | flops | bytes accessed | tf_op | source)
XLA Modules:
  0.0 172.3 jit_solution(222079052023049501)
XLA Ops:
  0.0 9.1 %first.1 = (s32[2,128]{1,0:T(2,128)S(1)}, f32[5120,128]{1,0:T(8,128)S(1)}) custom-call(s32[1,128]{1,0:T(1,128)} %bitcast.2, bf16[128,2048]{1,0:T(8,128)(2,1)} %xo_ref.1, bf16[2,2048]{1,0:T(2,128)(2,1)} %an_ref.3, bf16[2,2048,4608]{2,1,0:T(8,128)(2,1)} %wq_ref.5), custom_call_target="tpu_custom_call" | custom-call | tf_op jit(solution)/shard_map/first/pallas_call | solution.py:73
  9.1 18.7 %attn0.2 = (f32[64,2048]{1,0:T(8,128)S(1)}, bf16[3,8,576,512]{3,2,1,0:T(8,128)(2,1)S(1)}, bf16[4096,2048]{1,0:T(8,128)(2,1)S(1)}) custom-call(s32[2,128]{1,0:T(2,128)S(1)} %get-tuple-element.17.order_ref, f32[5120,128]{1,0:T(8,128)S(1)} %get-tuple-element.18.q_ref, bf16[2,128,576,512]{3,2,1,0:T(8,128)(2,1)} %bitcast.1.ct_ref, bf16[2,4096,2048]{2,1,0:T(8,128)(2,1)} %wo_ref.5), custom_call_target="tpu_custom_call" | custom-call | flops 20000000000 | bytes 41943040 | tf_op jit(solution)/shard_map/attn0/pallas_call | solution.py:211
  27.8 3.4 %collective-permute-start = (f32[64,2048]{1,0:T(8,128)S(1)}, f32[64,2048]{1,0:T(8,128)S(1)}, u32[]{:S(2)}, u32[]{:S(2)}) collective-permute-start(f32[64,2048]{1,0:T(8,128)S(1)} %get-tuple-element.22), channel_id=1, source_target_pairs={{0,4},{4,0},{1,5},{5,1},{2,6},{6,2},{3,7},{7,3}} | collective-permute-start | bytes 1572872 | tf_op jit(solution)/shard_map/ppermute | solution.py:496
  31.1 0.0 copy-start
  31.1 0.0 copy-start.1
  31.1 0.0 copy-start.2
  31.1 16.3 %attn0.3 = (f32[64,2048]{1,0:T(8,128)S(1)}, bf16[3,8,576,512]{3,2,1,0:T(8,128)(2,1)S(1)}) custom-call(s32[2,128]{1,0:T(2,128)S(1)} %get-tuple-element.17.order_ref, f32[5120,128]{1,0:T(8,128)S(1)} %get-tuple-element.18.q_ref, bf16[2,128,576,512]{3,2,1,0:T(8,128)(2,1)} %bitcast.1.ct_ref, ...), custom_call_target="tpu_custom_call", output_to_operand_aliasing={{1}: (4, {})} | custom-call | flops 20000000000 | bytes 41943040 | tf_op jit(solution)/shard_map/attn0/pallas_call | solution.py:211
  47.5 0.0 collective-permute-done.pb_ref
  47.5 0.0 copy-done
  47.5 0.0 copy-done.1
  47.5 0.0 copy-done.2
  47.5 46.2 %ffn0.1 = (bf16[64,2048]{1,0:T(8,128)(2,1)S(1)}, f32[5120,128]{1,0:T(8,128)S(1)}, bf16[4096,2048]{1,0:T(8,128)(2,1)S(1)}) custom-call(bf16[128,2048]{1,0:T(8,128)(2,1)S(1)} %copy-done, f32[64,2048]{1,0:T(8,128)S(1)} %get-tuple-element.21.pa_ref, f32[64,2048]{1,0:T(8,128)S(1)} %collective-permute-done.pb_ref, bf16[2,2048]{1,0:T(2,128)(2,1)S(1)} %copy-done.2, ...), custom_call_target="tpu_custom_call" | custom-call | tf_op jit(solution)/shard_map/ffn0/pallas_call | solution.py:470
  93.7 18.2 %attn1.2 = (f32[64,2048]{1,0:T(8,128)S(1)}, bf16[3,8,576,512]{3,2,1,0:T(8,128)(2,1)S(1)}) custom-call(s32[2,128]{1,0:T(2,128)S(1)} %get-tuple-element.17.order_ref, f32[5120,128]{1,0:T(8,128)S(1)} %get-tuple-element.24.q_ref, bf16[2,128,576,512]{3,2,1,0:T(8,128)(2,1)} %bitcast.1.ct_ref, bf16[4096,2048]{1,0:T(8,128)(2,1)S(1)} %get-tuple-element.25.wo_ref), custom_call_target="tpu_custom_call" | custom-call | flops 20000000000 | bytes 41943040 | tf_op jit(solution)/shard_map/attn1/pallas_call | solution.py:211
  111.9 0.8 collective-permute-start.1
  112.7 16.4 %attn1.3 = (f32[64,2048]{1,0:T(8,128)S(1)}, bf16[3,8,576,512]{3,2,1,0:T(8,128)(2,1)S(1)}) custom-call(s32[2,128]{1,0:T(2,128)S(1)} %get-tuple-element.17.order_ref, f32[5120,128]{1,0:T(8,128)S(1)} %get-tuple-element.24.q_ref, bf16[2,128,576,512]{3,2,1,0:T(8,128)(2,1)} %bitcast.1.ct_ref, ...), custom_call_target="tpu_custom_call", output_to_operand_aliasing={{1}: (4, {})} | custom-call | flops 20000000000 | bytes 41943040 | tf_op jit(solution)/shard_map/attn1/pallas_call | solution.py:211
  129.1 0.0 collective-permute-done.1.pb_ref
  129.1 42.4 %ffn1.1 = bf16[128,2048]{1,0:T(8,128)(2,1)S(1)} custom-call(bf16[64,2048]{1,0:T(8,128)(2,1)S(1)} %get-tuple-element.23.xo_ref, f32[64,2048]{1,0:T(8,128)S(1)} %get-tuple-element.27.pa_ref, f32[64,2048]{1,0:T(8,128)S(1)} %collective-permute-done.1.pb_ref, bf16[2,2048]{1,0:T(2,128)(2,1)S(1)} %copy-done.2, bf16[2,2048]{1,0:T(2,128)(2,1)S(1)} %copy-done.1, ...), custom_call_target="tpu_custom_call" | custom-call | tf_op jit(solution)/shard_map/ffn1/pallas_call | solution.py:470
  171.5 0.8 copy.16
Async XLA Ops:
  27.8 19.7 %collective-permute-start = (f32[64,2048]{1,0:T(8,128)S(1)}, f32[64,2048]{1,0:T(8,128)S(1)}, u32[]{:S(2)}, u32[]{:S(2)}) collective-permute-start(f32[64,2048]{1,0:T(8,128)S(1)} %get-tuple-element.22), channel_id=1, source_target_pairs={{0,4},{4,0},{1,5},{5,1},{2,6},{6,2},{3,7},{7,3}} | collective-permute-start | bytes 1572872 | tf_op jit(solution)/shard_map/ppermute | solution.py:496
  31.1 16.3 %copy-start = (bf16[128,2048]{1,0:T(8,128)(2,1)S(1)}, bf16[128,2048]{1,0:T(8,128)(2,1)}, u32[]{:S(2)}) copy-start(bf16[128,2048]{1,0:T(8,128)(2,1)} %xo_ref.1) | copy-start | bytes 1572868
  31.1 16.4 %copy-start.1 = (bf16[2,2048]{1,0:T(2,128)(2,1)S(1)}, bf16[2,2048]{1,0:T(2,128)(2,1)}, u32[]{:S(2)}) copy-start(bf16[2,2048]{1,0:T(2,128)(2,1)} %an_ref.3) | copy-start | bytes 24580
  31.1 16.4 %copy-start.2 = (bf16[2,2048]{1,0:T(2,128)(2,1)S(1)}, bf16[2,2048]{1,0:T(2,128)(2,1)}, u32[]{:S(2)}) copy-start(bf16[2,2048]{1,0:T(2,128)(2,1)} %fn_ref.3) | copy-start | bytes 24580
  111.9 17.2 %collective-permute-start.1 = (f32[64,2048]{1,0:T(8,128)S(1)}, f32[64,2048]{1,0:T(8,128)S(1)}, u32[]{:S(2)}, u32[]{:S(2)}) collective-permute-start(f32[64,2048]{1,0:T(8,128)S(1)} %get-tuple-element.28), channel_id=1, source_target_pairs={{0,4},{4,0},{1,5},{5,1},{2,6},{6,2},{3,7},{7,3}} | collective-permute-start | bytes 1572872 | tf_op jit(solution)/shard_map/ppermute | solution.py:496

commit v6 on v4

--- a/solution.py
+++ b/solution.py
@@ -16,9 +16,6 @@
 VMEM = pl.BlockSpec(memory_space=pltpu.VMEM)
 SMEM = pl.BlockSpec(memory_space=pltpu.SMEM)
 ANY = pl.BlockSpec(memory_space=pl.ANY)
-
-
-PAD = 256
 
 
 def _rmsnorm(v, w):
@@ -84,11 +81,11 @@
                         pltpu.SemaphoreType.DMA((3,))],
         compiler_params=pltpu.CompilerParams(vmem_limit_bytes=32 * 2 ** 20),
         name="first",
-    )(*[pltpu.with_memory_space_constraint(t, pltpu.HBM) for t in (lens.reshape(1, nb), x, an, wq)])
-
-
-def _attn_kernel(layer, off, nh, G, NS, order_ref, q_ref, ct_ref, wo_ref, out_ref, *rest):
-    if off == 0:
+    )(*[pltpu.with_memory_space_constraint(t, pltpu.HBM) for t in (lens.reshape(1, nb), x, an)], wq)
+
+
+def _attn_kernel(layer, off, load, nh, G, NS, order_ref, q_ref, ct_ref, wo_ref, out_ref, *rest):
+    if load:
         wbuf, buf, sems, o_s, oflat, wsems = rest
     else:
         buf, sems, o_s, oflat = rest
@@ -140,7 +137,7 @@
         @pl.when(g + NS - 1 < ng)
         def _():
             start(g + NS - 1)
-        if off == 0:
+        if load:
             wcopy(g).start()
         c = chunks(g)
         slot = lax.rem(g, NS)
@@ -172,7 +169,7 @@
         for i in range(LAT // 128):
             c = h * LAT + i * 128
             oflat[:, c:c + 128] = o_s[pl.ds((h * (LAT // 128) + i) * nb, nb), :].astype(BF)
-    for g in range(ng if off == 0 else 0):
+    for g in range(ng if load else 0):
         wcopy(g).wait()
     nblk = 1024
 
@@ -187,16 +184,17 @@
     kv, s_len = ct.shape[2:]
     nb = order.shape[1] // 2
     hid, d = wo.shape[-2:]
+    load = wo.ndim == 3
     part = jax.ShapeDtypeStruct((nb, d), F32)
     return pl.pallas_call(
-        functools.partial(_attn_kernel, layer, off, nh, G, NS),
-        out_shape=[part, jax.ShapeDtypeStruct((hid, d), BF)] if off == 0 else part,
-        in_specs=[SMEM, VMEM, ANY, ANY if off == 0 else VMEM],
-        out_specs=[VMEM, VMEM] if off == 0 else VMEM,
+        functools.partial(_attn_kernel, layer, off, load, nh, G, NS),
+        out_shape=[part, jax.ShapeDtypeStruct((hid, d), BF)] if load else part,
+        in_specs=[SMEM, VMEM, ANY, ANY if load else VMEM],
+        out_specs=[VMEM, VMEM] if load else VMEM,
         scratch_shapes=[
             pltpu.VMEM((NS, G, kv, s_len), BF), pltpu.SemaphoreType.DMA((NS, G)),
             pltpu.VMEM((LAT // 128 * nb * nh, 128), F32), pltpu.VMEM((nb, hid), BF),
-        ] + ([pltpu.SemaphoreType.DMA((nb // G,))] if off == 0 else []),
+        ] + ([pltpu.SemaphoreType.DMA((nb // G,))] if load else []),
         compiler_params=pltpu.CompilerParams(vmem_limit_bytes=24 * 2 ** 20),
         cost_estimate=pl.CostEstimate(flops=20 * 10 ** 9, bytes_accessed=40 * 2 ** 20, transcendentals=0),
         name=f"attn{layer}",
@@ -212,14 +210,14 @@
 HALF = 64
 
 
-def _ffn_kernel(layer, last, nh, xo_ref, pa_ref, pb_ref, fn_ref, an_ref, w1_ref, w3_ref, w2_ref, wq_ref, *rest):
+def _ffn_kernel(layer, last, nh, xo_ref, pa_ref, pb_ref, fn_ref, an_ref, w1_ref, w3_ref, w2_ref, wq_ref, wo_ref, *rest):
     if last:
         out_ref, rest = rest[0], rest[1:]
     else:
-        xn_ref, q_ref, rest = rest[0], rest[1], rest[2:]
-    (w13, w2v, wqv, gbuf, ybuf, sbuf, abuf, xp, xall,
+        xn_ref, q_ref, won_ref, rest = rest[0], rest[1], rest[2], rest[3:]
+    (w13, w2b, gbuf, ybuf, sbuf, abuf, xp, xall,
      r1x_own, r1x_y, r1y_own, r1y_x, r2x, r2y,
-     wsem, w2sem, wqsem, ss, rs) = rest
+     wsem, w2sem, wqsem, wosem, ss, rs) = rest
     tp = lax.axis_index("tp")
     dp = lax.axis_index("dp")
     xi, ci = lax.div(dp, 2), lax.rem(dp, 2)
@@ -238,19 +236,17 @@
             wcopies.append(pltpu.make_async_copy(
                 w.at[layer, :, pl.ds(j * 128, 128)], w13.at[:, pl.ds(j * 256 + i * 128, 128)],
                 wsem.at[j, i]))
-    w2copy = pltpu.make_async_copy(w2_ref.at[layer], w2v.at[:, pl.ds(0, w2_ref.shape[2])], w2sem)
+    w2copy = pltpu.make_async_copy(w2_ref.at[layer], w2b.at[pl.ds(0, w2_ref.shape[1]), pl.ds(0, w2_ref.shape[2])], w2sem)
     for cp in wcopies:
         cp.start()
     w2copy.start()
     nj = nh // 2
     if not last:
         kv2 = wq_ref.shape[2] // nj
-        dst = [w13.at[:, pl.ds(j * kv2, kv2)] if j < 2 else wqv.at[j - 2, :, pl.ds(0, kv2)]
-               for j in range(nj)]
+        dst = [(w13 if j < 2 else w2b).at[:, pl.ds(j % 2 * kv2, kv2)] for j in range(nj)]
         wqcopies = [pltpu.make_async_copy(wq_ref.at[layer + 1, :, pl.ds(j * kv2, kv2)], dst[j], wqsem.at[j])
                     for j in range(nj)]
-        for cp in wqcopies[2:]:
-            cp.start()
+        wocopy = pltpu.make_async_copy(wo_ref.at[layer + 1], won_ref, wosem)
 
     count = [16]
 
@@ -358,12 +354,16 @@
 
         a = abuf[...]
         for q in QORDER:
-            y = jnp.dot(a, w2v[:, q * W:(q + 1) * W], preferred_element_type=F32)
+            y = jnp.dot(a, w2b[0:w2_ref.shape[1], q * W:(q + 1) * W], preferred_element_type=F32)
             ybuf[k, :, :, :, q * W:(q + 1) * W] = y.reshape(2, 2, 32, W)
             sib_y(k, q).start()
         return carry
 
     lax.fori_loop(0, 4, chunk, 0)
+    if not last:
+        for cp in wqcopies[2:]:
+            cp.start()
+        wocopy.start()
     for q in QORDER:
         combine(3, q)
         for p in PS:
@@ -409,6 +409,8 @@
         for j, cp in enumerate(wqcopies):
             cp.wait()
             _project(h, dst[j][...], j, q_ref, 2 * HALF, kv2 // 2)
+    if not last:
+        wocopy.wait()
     for cp in [own_sib, relay_x, relay_y, *own_x.values(), *own_y.values(), *sib_g.values(),
                *st1_x.values(), *st1_y.values(), *st1_dx.values(), *st1_dy.values(),
                *st2_x.values(), *st2_y.values(), *xg.values()]:
@@ -421,7 +423,7 @@
 NCOPY = 16 + 10 + 4 + 8 + 8 + 8
 
 
-def _ffn(layer, last, nh, xo, pa, pb, fn, an, w1, w3, w2, wq):
+def _ffn(layer, last, nh, xo, pa, pb, fn, an, w1, w3, w2, wq, wo):
     rows, d = pa.shape
     f = w1.shape[2]
     kv = wq.shape[2] // nh
@@ -429,29 +431,29 @@
         out_shape = [jax.ShapeDtypeStruct((2 * rows, d), BF)]
     else:
         out_shape = [jax.ShapeDtypeStruct((rows, d), BF),
-                     jax.ShapeDtypeStruct((-(-kv // 128) * 2 * rows * nh, 128), F32)]
+                     jax.ShapeDtypeStruct((-(-kv // 128) * 2 * rows * nh, 128), F32),
+                     jax.ShapeDtypeStruct(wo.shape[1:], BF)]
     NA, NB = len(A), len(B)
     scratch = [
-        pltpu.VMEM((d, 2 * f), BF), pltpu.VMEM((f, d + PAD), BF),
-        pltpu.VMEM((1, 16, 128) if last else (nh // 2 - 2, d, 2 * kv + 128), BF),
+        pltpu.VMEM((d, 2 * f), BF), pltpu.VMEM((f, d) if last else (d, 4 * kv), BF),
         pltpu.VMEM((4, 2, 2, 32, d), BF), pltpu.VMEM((4, 2, 2, 32, d), F32), pltpu.VMEM((4, 2, 32, d), F32),
         pltpu.VMEM((128, f), BF), pltpu.VMEM((rows, d), BF), pltpu.VMEM((2 * rows, d), BF),
         pltpu.VMEM((2, 32, NA * W), F32), pltpu.VMEM((2, NA, 32, W), F32),
         pltpu.VMEM((2, 32, NB * W), F32), pltpu.VMEM((2, NB, 32, W), F32),
         pltpu.VMEM((2, NB, 32, W), F32), pltpu.VMEM((2, NA, 32, W), F32),
         pltpu.SemaphoreType.DMA((f // 128, 2)), pltpu.SemaphoreType.DMA, pltpu.SemaphoreType.DMA((nh // 2,)),
-        pltpu.SemaphoreType.DMA((NCOPY,)), pltpu.SemaphoreType.DMA((NCOPY,)),
+        pltpu.SemaphoreType.DMA, pltpu.SemaphoreType.DMA((NCOPY,)), pltpu.SemaphoreType.DMA((NCOPY,)),
     ]
     return pl.pallas_call(
         functools.partial(_ffn_kernel, layer, last, nh),
         out_shape=out_shape,
-        in_specs=[VMEM, VMEM, VMEM, VMEM, VMEM, ANY, ANY, ANY, ANY],
+        in_specs=[VMEM, VMEM, VMEM, VMEM, VMEM, ANY, ANY, ANY, ANY, ANY],
         out_specs=[VMEM] * len(out_shape),
         scratch_shapes=scratch,
         compiler_params=pltpu.CompilerParams(collective_id=layer, has_side_effects=True,
-                                             vmem_limit_bytes=48 * 2 ** 20),
+                                             vmem_limit_bytes=65 * 2 ** 19),
         name=f"ffn{layer}",
-    )(xo, pa, pb, fn, an, w1, w3, w2, wq)
+    )(xo, pa, pb, fn, an, w1, w3, w2, wq, wo)
 
 
 def solution(mesh):
@@ -460,16 +462,20 @@
         n_layers, _, s_len, kv = cache.shape
         nh = wq.shape[2] // kv
         ct = jnp.swapaxes(cache, 2, 3)
+        ct, wq, wo, w1, w3, w2 = [pltpu.with_memory_space_constraint(t, pltpu.HBM) for t in (ct, wq, wo, w1, w3, w2)]
         order, q = _first(lengths, x, attn_norm, wq, nh)
         for l in range(n_layers):
             last = l == n_layers - 1
-            pa, wo_l = _attention(l, 0, q, ct, order, wo, nh)
+            if l == 0:
+                pa, wo_l = _attention(l, 0, q, ct, order, wo, nh)
+            else:
+                pa = _attention(l, 0, q, ct, order, wo_l, nh)
             pa = lax.ppermute(pa, 'tp', [(0, 1), (1, 0)])
             pb = _attention(l, nb // 2, q, ct, order, wo_l, nh)
-            res = _ffn(l, last, nh, x, pb, pa, ffn_norm, attn_norm, w1, w3, w2, wq)
+            res = _ffn(l, last, nh, x, pb, pa, ffn_norm, attn_norm, w1, w3, w2, wq, wo)
             if last:
                 return res[0]
-            x, q = res
+            x, q, wo_l = res
 
     in_specs = (
         P('dp', None),

time: 175 us -> 173 us (0.989)
  starting transfers between devices: 10.2 us -> 4.07 us
  Pallas kernels: 163 us -> 168 us
    ppermute x2, starting transfers between devices: 10.2 us -> 4.07 us  [body(): pa = lax.ppermute(pa, 'tp', [(0, 1), (1, 0)])]
    pallas_call x2, Pallas kernels: 83.1 us -> 87.8 us  [_ffn(): pl.pallas_call(functools.partial(_ffn_kernel, layer, last, nh), out_shape...]
  transfers between devices with their start and end apart: 2 -> 2, of which waited for: 0 -> 0; matrix products, arithmetic and copies ran while one was open for 0% -> 0% of each run, Pallas kernels for 21% -> 20%
where the time goes in v6:
time: 173 us
  Pallas kernels  168 us (97%)
  starting transfers between devices  4.07 us (2%)
    pallas_call x2, Pallas kernels, _ffn(): pl.pallas_call(functools.partial(_ffn_kernel, layer, last, nh), out_shape...  87.8 us
    pallas_call x4, Pallas kernels, _attention(): pl.pallas_call(functools.partial(_attn_kernel, layer, off, load, nh, G, N...  70.8 us
    pallas_call x1, Pallas kernels, _first(): pl.pallas_call(_first_kernel, out_shape=[jax.ShapeDtypeStruct((2, nb), jn...  9.07 us
    ppermute x2, starting transfers between devices, body(): pa = lax.ppermute(pa, 'tp', [(0, 1), (1, 0)])  4.07 us
  transfers between devices with their start and end apart: 2, of which 0 were waited for; matrix products, arithmetic and copies ran while one was open for 0% of the time, Pallas kernels for 20%

profile of v6, /device:TPU:0, one launch (start us, length us, event | category | flops | bytes accessed | tf_op | source)
XLA Modules:
  0.0 172.6 jit_solution(16086179895994656426)
XLA Ops:
  0.0 9.1 %first.1 = (s32[2,128]{1,0:T(2,128)S(1)}, f32[5120,128]{1,0:T(8,128)S(1)}) custom-call(s32[1,128]{1,0:T(1,128)} %bitcast.2, bf16[128,2048]{1,0:T(8,128)(2,1)} %xo_ref.1, bf16[2,2048]{1,0:T(2,128)(2,1)} %an_ref.3, bf16[2,2048,4608]{2,1,0:T(8,128)(2,1)} %wq_ref.5), custom_call_target="tpu_custom_call" | custom-call | tf_op jit(solution)/shard_map/first/pallas_call | solution.py:73
  9.1 17.8 %attn0.2 = (f32[64,2048]{1,0:T(8,128)S(1)}, bf16[4096,2048]{1,0:T(8,128)(2,1)S(1)}) custom-call(s32[2,128]{1,0:T(2,128)S(1)} %get-tuple-element.12.order_ref, f32[5120,128]{1,0:T(8,128)S(1)} %get-tuple-element.13.q_ref, bf16[2,128,576,512]{3,2,1,0:T(8,128)(2,1)} %bitcast.1.ct_ref, bf16[2,4096,2048]{2,1,0:T(8,128)(2,1)} %wo_ref.5), custom_call_target="tpu_custom_call" | custom-call | flops 20000000000 | bytes 41943040 | tf_op jit(solution)/shard_map/attn0/pallas_call | solution.py:189
  26.9 3.4 %collective-permute-start = (f32[64,2048]{1,0:T(8,128)S(1)}, f32[64,2048]{1,0:T(8,128)S(1)}, u32[]{:S(2)}, u32[]{:S(2)}) collective-permute-start(f32[64,2048]{1,0:T(8,128)S(1)} %get-tuple-element.15), channel_id=1, source_target_pairs={{0,4},{4,0},{1,5},{5,1},{2,6},{6,2},{3,7},{7,3}} | collective-permute-start | bytes 1572872 | tf_op jit(solution)/shard_map/ppermute | solution.py:473
  30.2 0.0 copy-start
  30.2 0.0 copy-start.1
  30.2 0.0 copy-start.2
  30.2 17.5 %attn0.3.pa_ref = f32[64,2048]{1,0:T(8,128)S(1)} custom-call(s32[2,128]{1,0:T(2,128)S(1)} %get-tuple-element.12.order_ref, f32[5120,128]{1,0:T(8,128)S(1)} %get-tuple-element.13.q_ref, bf16[2,128,576,512]{3,2,1,0:T(8,128)(2,1)} %bitcast.1.ct_ref, bf16[4096,2048]{1,0:T(8,128)(2,1)S(1)} %get-tuple-element.14.wo_ref), custom_call_target="tpu_custom_call" | custom-call | flops 20000000000 | bytes 41943040 | tf_op jit(solution)/shard_map/attn0/pallas_call | solution.py:189
  47.8 0.0 collective-permute-done.pb_ref
  47.8 0.0 copy-done
  47.8 0.0 copy-done.1
  47.8 0.0 copy-done.2
  47.8 45.3 %ffn0.1 = (bf16[64,2048]{1,0:T(8,128)(2,1)S(1)}, f32[5120,128]{1,0:T(8,128)S(1)}, bf16[4096,2048]{1,0:T(8,128)(2,1)S(1)}) custom-call(bf16[128,2048]{1,0:T(8,128)(2,1)S(1)} %copy-done, f32[64,2048]{1,0:T(8,128)S(1)} %attn0.3.pa_ref, f32[64,2048]{1,0:T(8,128)S(1)} %collective-permute-done.pb_ref, bf16[2,2048]{1,0:T(2,128)(2,1)S(1)} %copy-done.2, ...), custom_call_target="tpu_custom_call" | custom-call | tf_op jit(solution)/shard_map/ffn0/pallas_call | solution.py:447
  93.1 17.8 %attn1.3 = f32[64,2048]{1,0:T(8,128)S(1)} custom-call(s32[2,128]{1,0:T(2,128)S(1)} %get-tuple-element.12.order_ref, f32[5120,128]{1,0:T(8,128)S(1)} %get-tuple-element.17.q_ref, bf16[2,128,576,512]{3,2,1,0:T(8,128)(2,1)} %bitcast.1.ct_ref, bf16[4096,2048]{1,0:T(8,128)(2,1)S(1)} %get-tuple-element.18.wo_ref), custom_call_target="tpu_custom_call" | custom-call | flops 20000000000 | bytes 41943040 | tf_op jit(solution)/shard_map/attn1/pallas_call | solution.py:189
  110.9 0.7 collective-permute-start.1
  111.7 17.6 %attn1.2.pa_ref = f32[64,2048]{1,0:T(8,128)S(1)} custom-call(s32[2,128]{1,0:T(2,128)S(1)} %get-tuple-element.12.order_ref, f32[5120,128]{1,0:T(8,128)S(1)} %get-tuple-element.17.q_ref, bf16[2,128,576,512]{3,2,1,0:T(8,128)(2,1)} %bitcast.1.ct_ref, bf16[4096,2048]{1,0:T(8,128)(2,1)S(1)} %get-tuple-element.18.wo_ref), custom_call_target="tpu_custom_call" | custom-call | flops 20000000000 | bytes 41943040 | tf_op jit(solution)/shard_map/attn1/pallas_call | solution.py:189
  129.3 0.0 collective-permute-done.1.pb_ref
  129.3 42.5 %ffn1.1 = bf16[128,2048]{1,0:T(8,128)(2,1)S(1)} custom-call(bf16[64,2048]{1,0:T(8,128)(2,1)S(1)} %get-tuple-element.16.xo_ref, f32[64,2048]{1,0:T(8,128)S(1)} %attn1.2.pa_ref, f32[64,2048]{1,0:T(8,128)S(1)} %collective-permute-done.1.pb_ref, bf16[2,2048]{1,0:T(2,128)(2,1)S(1)} %copy-done.2, bf16[2,2048]{1,0:T(2,128)(2,1)S(1)} %copy-done.1, ...), custom_call_target="tpu_custom_call" | custom-call | tf_op jit(solution)/shard_map/ffn1/pallas_call | solution.py:447
  171.8 0.8 copy.12
Async XLA Ops:
  26.9 20.9 %collective-permute-start = (f32[64,2048]{1,0:T(8,128)S(1)}, f32[64,2048]{1,0:T(8,128)S(1)}, u32[]{:S(2)}, u32[]{:S(2)}) collective-permute-start(f32[64,2048]{1,0:T(8,128)S(1)} %get-tuple-element.15), channel_id=1, source_target_pairs={{0,4},{4,0},{1,5},{5,1},{2,6},{6,2},{3,7},{7,3}} | collective-permute-start | bytes 1572872 | tf_op jit(solution)/shard_map/ppermute | solution.py:473
  30.2 17.6 %copy-start = (bf16[128,2048]{1,0:T(8,128)(2,1)S(1)}, bf16[128,2048]{1,0:T(8,128)(2,1)}, u32[]{:S(2)}) copy-start(bf16[128,2048]{1,0:T(8,128)(2,1)} %xo_ref.1) | copy-start | bytes 1572868
  30.2 17.6 %copy-start.1 = (bf16[2,2048]{1,0:T(2,128)(2,1)S(1)}, bf16[2,2048]{1,0:T(2,128)(2,1)}, u32[]{:S(2)}) copy-start(bf16[2,2048]{1,0:T(2,128)(2,1)} %an_ref.3) | copy-start | bytes 24580
  30.2 17.6 %copy-start.2 = (bf16[2,2048]{1,0:T(2,128)(2,1)S(1)}, bf16[2,2048]{1,0:T(2,128)(2,1)}, u32[]{:S(2)}) copy-start(bf16[2,2048]{1,0:T(2,128)(2,1)} %fn_ref.3) | copy-start | bytes 24580
  110.9 18.3 %collective-permute-start.1 = (f32[64,2048]{1,0:T(8,128)S(1)}, f32[64,2048]{1,0:T(8,128)S(1)}, u32[]{:S(2)}, u32[]{:S(2)}) collective-permute-start(f32[64,2048]{1,0:T(8,128)S(1)} %attn1.3), channel_id=1, source_target_pairs={{0,4},{4,0},{1,5},{5,1},{2,6},{6,2},{3,7},{7,3}} | collective-permute-start | bytes 1572872 | tf_op jit(solution)/shard_map/ppermute | solution.py:473
